TPU v7x, 128 devices: a whole 4x4x4 slice. The times are simulated.
128 devices in a mesh: chord: 8 (over y_lo, z), span: 16 (over x, y_hi, core).
Axes of the slice: x: 4, y: 4 (y_hi: 2, y_lo: 2; y = y_hi * 2 + y_lo), z: 4, core: 2. Of those that a mesh axis runs over, the one named last changes fastest.
Arguments:
- state: float32 [5, 125, 32, 32, 128], P(None, None, 'chord', 'span'), may hold values from -10 to 10
Outputs:
- residual: float32 [5, 125, 32, 32, 128], P(None, None, 'chord', 'span')
- viscosity: float32 [125, 32, 32, 128], P(None, 'chord', 'span')
All inputs are finite; a program needn't handle non-finite values.
Results may differ from a plain program's by a relative error of at most 0.0001.
Values sent between devices are 32-bit elements; how exact they have to be, the bound alone decides.
No kernel may reach another device: no remote copies, remote signals or barrier semaphores. Data moves between devices by JAX's collectives and lax.ppermute only.
A program may use at most 128 MiB of HBM per device.

v0:
```python
import functools
import math

import jax
import jax.numpy as jnp
import numpy as np
from jax import lax
from jax.experimental import pallas as pl
from jax.experimental.pallas import tpu as pltpu
from jax.sharding import PartitionSpec as P

EPS_SCALE = 0.01
SENSOR_CENTRE = -3.0
SENSOR_WIDTH = 1.5
RATIO_FLOOR = 1e-06
ENERGY_EPS = 1e-06
GAUSS_NODES = [-0.906179845938664, -0.5384693101056831, 0.0, 0.5384693101056831, 0.906179845938664]
GAUSS_WEIGHTS = [
    0.2369268850561891,
    0.4786286704993665,
    0.5688888888888889,
    0.4786286704993665,
    0.2369268850561891,
]


def legendre_values(points):
    values = [np.ones(points.shape), np.array(points)]
    for order in range(1, 5):
        values.append(
            ((2 * order + 1) * points * values[order] - order * values[order - 1]) / (order + 1)
        )
    return values


def line_tables():
    line_nodes = np.array(GAUSS_NODES)
    quadrature_weights = np.array(GAUSS_WEIGHTS)
    barycentric = np.array(
        [
            1.0 / np.prod([line_nodes[j] - line_nodes[k] for k in range(5) if k != j])
            for j in range(5)
        ]
    )
    derivative = np.zeros((5, 5))
    for i in range(5):
        for j in range(5):
            if i != j:
                derivative[i, j] = barycentric[j] / barycentric[i] / (line_nodes[i] - line_nodes[j])
        derivative[i, i] = -np.sum(derivative[i])
    left_values = np.ones(5)
    right_values = np.ones(5)
    for j in range(5):
        for k in range(5):
            if k != j:
                left_values[j] *= (-1.0 - line_nodes[k]) / (line_nodes[j] - line_nodes[k])
                right_values[j] *= (1.0 - line_nodes[k]) / (line_nodes[j] - line_nodes[k])
    legendre = legendre_values(line_nodes)
    fourth_slope = 7.0 * legendre[3] + 3.0 * legendre[1]
    fifth_slope = 9.0 * legendre[4] + 5.0 * legendre[2] + legendre[0]
    modal = np.zeros((5, 5))
    for k in range(5):
        modal[k, :] = quadrature_weights * math.sqrt((2 * k + 1) / 2.0) * legendre[k]
    return (line_nodes, derivative, left_values, right_values, fourth_slope, fifth_slope, modal)


NODES, DERIV, LEFT, RIGHT, SLOPE4, SLOPE5, MODAL = line_tables()
CORR_L = 0.5 * (SLOPE4 - SLOPE5)
CORR_R = 0.5 * (SLOPE4 + SLOPE5)
OWN = DERIV - 0.5 * (np.outer(CORR_L, LEFT) + np.outer(CORR_R, RIGHT))
ROWS, LANES = 8, 128
NV, NF = 5, 25
SPAN_V, CHORD_V = 13, 7
SPAN_N, CHORD_N = NV * SPAN_V, NV * CHORD_V


def mul(scale, x):
    return float(scale) * x


def even_odd(x):
    return (x[0] + x[4], x[1] + x[3], x[0] - x[4], x[1] - x[3], x[2])


def traces(parts):
    e0, e1, o0, o1, c = parts
    even = (
        mul(0.5 * (LEFT[0] + LEFT[4]), e0) + mul(0.5 * (LEFT[1] + LEFT[3]), e1) + mul(LEFT[2], c)
    )
    odd = mul(0.5 * (LEFT[0] - LEFT[4]), o0) + mul(0.5 * (LEFT[1] - LEFT[3]), o1)
    return (even + odd, even - odd)


def slope(parts, total, diff):
    e0, e1, o0, o1, c = parts
    even, odd = [], []
    for i in range(3):
        even.append(
            mul(0.5 * (OWN[i, 0] - OWN[i, 4]), o0)
            + mul(0.5 * (OWN[i, 1] - OWN[i, 3]), o1)
            + mul(0.25 * SLOPE5[i], diff)
        )
    for i in range(2):
        odd.append(
            mul(0.5 * (OWN[i, 0] + OWN[i, 4]), e0)
            + mul(0.5 * (OWN[i, 1] + OWN[i, 3]), e1)
            + (mul(OWN[i, 2], c) + mul(0.25 * SLOPE4[i], total))
        )
    return [
        even[0] + odd[0],
        even[1] + odd[1],
        even[2],
        even[1] - odd[1],
        even[0] - odd[0],
    ]


def modal_line(x):
    e0, e1, o0, o1, c = even_odd(x)
    out = []
    for k in range(5):
        if k % 2 == 0:
            out.append(mul(MODAL[k, 0], e0) + mul(MODAL[k, 1], e1) + mul(MODAL[k, 2], c))
        else:
            out.append(mul(MODAL[k, 0], o0) + mul(MODAL[k, 1], o1))
    return out


def line_points(axis, f):
    a, b = f // 5, f % 5
    if axis == 0:
        return [25 * k + 5 * a + b for k in range(5)]
    if axis == 1:
        return [25 * a + 5 * k + b for k in range(5)]
    return [25 * a + 5 * b + k for k in range(5)]


def row_ids():
    rows = lax.broadcasted_iota(jnp.int32, (ROWS, LANES), 0)
    return (rows // 2, rows % 2)


def lane_ids():
    return lax.broadcasted_iota(jnp.int32, (ROWS, LANES), 1)


def up_rows(x, n):
    n = n % ROWS
    return x if n == 0 else pltpu.roll(x, n, 0)


def splat_flag(flag):
    return jnp.full((ROWS, LANES), flag.astype(jnp.int32), jnp.int32) > 0


def even_span():
    return splat_flag(lax.axis_index("span") % 2 == 0)


def even_chord():
    return splat_flag(lax.axis_index("chord") % 2 == 0)


def pack_span(out_of, is_low, even, first_ref, second_ref, base):
    for m in range(SPAN_V):
        f0 = out_of(2 * m)
        f1 = out_of(2 * m + 1) if 2 * m + 1 < NF else f0
        up = jnp.where(is_low, up_rows(f0, -1), f1)
        down = jnp.where(is_low, f0, up_rows(f1, 1))
        first_ref[base + m] = jnp.where(even, up, down)
        second_ref[base + m] = jnp.where(even, down, up)


def pack_chord(out_of, i, even, first_ref, second_ref, base):
    for m in range(CHORD_V):
        up = down = None
        for q in range(4):
            f = 4 * m + q
            if f >= NF:
                continue
            trace = out_of(f)
            u, d = up_rows(trace, 2 * q - 6), up_rows(trace, 2 * q)
            up = u if up is None else jnp.where(i == q, u, up)
            down = d if down is None else jnp.where(i == q, d, down)
        first_ref[base + m] = jnp.where(even, up, down)
        second_ref[base + m] = jnp.where(even, down, up)


def open_span(below, above, q, is_low):
    if q == 0:
        return jnp.where(is_low, below, up_rows(above, 1))
    return jnp.where(is_low, up_rows(below, -1), above)


def open_chord(below, above, q, i):
    return jnp.where(i == 0, up_rows(below, -2 * q), up_rows(above, 6 - 2 * q))


def leave_kernel(state, so, se, co, ce, eps_ref, work):
    i, j = row_ids()
    is_low, first_row = j == 0, i == 0
    es, ec = even_span(), even_chord()

    def one(v, carry):
        def leaving(axis, mask, f):
            left, right = traces(even_odd([state[v, p] for p in line_points(axis, f)]))
            return jnp.where(mask, left, right)

        pack_span(functools.partial(leaving, 1, is_low), is_low, es, se, so, v * SPAN_V)
        pack_chord(functools.partial(leaving, 0, first_row), i, ec, ce, co, v * CHORD_V)
        return carry

    lax.fori_loop(0, NV, one, 0)
    for axis in range(2):
        source = state.at[0] if axis == 0 else work
        for f in range(NF):
            points = line_points(axis, f)
            for p, value in zip(points, modal_line([source[p] for p in points])):
                work[p] = value
    low_sums, high_sums = [], []
    for f in range(NF):
        a, b = f // 5, f % 5
        low, high = None, None
        for k, value in enumerate(modal_line([work[p] for p in line_points(2, f)])):
            square = value * value
            if a == 4 or b == 4 or k == 4:
                high = square if high is None else high + square
            else:
                low = square if low is None else low + square
        if low is not None:
            low_sums.append(low)
        high_sums.append(high)

    def tree(values):
        while len(values) > 1:
            values = [
                values[n] + values[n + 1] if n + 1 < len(values) else values[n]
                for n in range(0, len(values), 2)
            ]
        return values[0]

    high_part = tree(high_sums)
    total = (tree(low_sums) + high_part) + ENERGY_EPS
    level = jnp.log(jnp.maximum(high_part / total, RATIO_FLOOR)) * (1.0 / math.log(10.0))
    ramp = jnp.clip((level - SENSOR_CENTRE) / SENSOR_WIDTH, -1.0, 1.0)
    eps = EPS_SCALE * 0.5 * (1.0 + jnp.sin(0.5 * math.pi * ramp))
    eps_ref[...] = eps
    for ref, at in ((so, SPAN_N), (se, SPAN_N), (co, CHORD_N), (ce, CHORD_N)):
        ref[at] = eps


def corner_kernel(rce, rco, cor):
    ec = even_chord()
    first, second = rce[CHORD_N], rco[CHORD_N]
    cor[0] = jnp.where(ec, second, first)
    cor[1] = jnp.where(ec, first, second)


def neighbours_chord(left, right, sign, i):
    first = (lax.axis_index("chord") == 0).astype(jnp.float32) * sign
    last = (lax.axis_index("chord") == lax.axis_size("chord") - 1).astype(jnp.float32) * sign
    before = jnp.where(i == 0, left * first, up_rows(right, 2))
    after = jnp.where(i == 3, right * last, up_rows(left, -2))
    return (before + after, after - before)


def neighbours_span(left, right, is_low, sign_row):
    inner = jnp.where(is_low, up_rows(left, -1), up_rows(right, 1))
    return (inner, inner * sign_row)


def neighbours_normal(left, right, sign, lane):
    before = jnp.where(lane == 0, mul(sign, left), pltpu.roll(right, 1, 1))
    after = jnp.where(lane == LANES - 1, mul(sign, right), pltpu.roll(left, LANES - 1, 1))
    return (before + after, after - before)


def gradient_kernel(state, gc, gs, gn, total_ref, diff_ref):
    i, j = row_ids()
    lane = lane_ids()
    is_low = j == 0
    sign_row = jnp.where(is_low, 1.0, -1.0)

    def one(v, carry):
        def lines(axis, f):
            return even_odd([state[v, p] for p in line_points(axis, f)])

        for f in range(NF):
            left, right = traces(lines(2, f))
            total_ref[f], diff_ref[f] = neighbours_normal(left, right, 1.0, lane)
        for axis, ref in ((0, gc), (1, gs), (2, gn)):
            for f in range(NF):
                parts = lines(axis, f)
                if axis == 2:
                    total, diff = total_ref[f], diff_ref[f]
                else:
                    left, right = traces(parts)
                    if axis == 0:
                        total, diff = neighbours_chord(left, right, 1.0, i)
                    else:
                        total, diff = neighbours_span(left, right, is_low, sign_row)
                for p, value in zip(line_points(axis, f), slope(parts, total, diff)):
                    ref[v, p] = value
        return carry

    lax.fori_loop(0, NV, one, 0)


def viscosity_into(visc, own, below, above, before, after, cb, ca):
    i, j = row_ids()
    lane = lane_ids()
    is_low = j == 0

    def chord_pair(mid, low, high):
        under = up_rows(jnp.where(i == 3, low, mid), 2)
        over = up_rows(jnp.where(i == 0, high, mid), -2)
        return (jnp.maximum(mid, under), jnp.maximum(mid, over))

    mids = chord_pair(own, below, above)
    befores = chord_pair(before, cb[0], cb[1])
    afters = chord_pair(after, ca[0], ca[1])
    corners = {}
    for x in range(2):
        mid, low, high = mids[x], befores[x], afters[x]
        under = jnp.where(is_low, up_rows(low, -1), up_rows(mid, 1))
        over = jnp.where(is_low, up_rows(mid, -1), up_rows(high, 1))
        for y, value in enumerate((jnp.maximum(mid, under), jnp.maximum(mid, over))):
            low_z = jnp.where(lane == 0, value, pltpu.roll(value, 1, 1))
            high_z = jnp.where(lane == LANES - 1, value, pltpu.roll(value, LANES - 1, 1))
            corners[x, y, 0] = jnp.maximum(value, low_z)
            corners[x, y, 1] = jnp.maximum(value, high_z)
    halves = [((1.0 - x) / 2.0, (1.0 + x) / 2.0) for x in NODES]
    for a in range(5):
        plane = {
            (y, z): mul(halves[a][0], corners[0, y, z]) + mul(halves[a][1], corners[1, y, z])
            for y in range(2)
            for z in range(2)
        }
        for b in range(5):
            low, high = (
                mul(halves[b][0], plane[0, z]) + mul(halves[b][1], plane[1, z]) for z in range(2)
            )
            for c in range(5):
                visc[25 * a + 5 * b + c] = mul(halves[c][0], low) + mul(halves[c][1], high)


def span_flux_kernel(gs, eps, rcse, rcso, rse, rso, rce, rco, visc, fs, bso, bse):
    i, j = row_ids()
    is_low = j == 0
    es, ec = even_span(), even_chord()

    def sides(even, first, second):
        return (jnp.where(even, second, first), jnp.where(even, first, second))

    below, above = sides(ec, rce[CHORD_N], rco[CHORD_N])
    before, after = sides(es, rse[SPAN_N], rso[SPAN_N])
    low = [sides(es, rcse[n], rcso[n]) for n in range(2)]
    viscosity_into(
        visc, eps[...], below, above, before, after, (low[0][0], low[1][0]), (low[0][1], low[1][1])
    )
    weights = [jnp.where(is_low, float(0.5 * CORR_L[k]), float(0.5 * CORR_R[k])) for k in range(5)]

    def one(v, carry):
        received = {}

        def leaving(f):
            m, q = f // 2, f % 2
            if m not in received:
                base = v * SPAN_V + m
                received[m] = sides(es, rse[base], rso[base])
            edge = open_span(received[m][0], received[m][1], q, is_low)
            values = []
            for k, p in enumerate(line_points(1, f)):
                value = visc[p] * (gs[v, p] + weights[k] * edge)
                fs[v, p] = value
                values.append(value)
            left, right = traces(even_odd(values))
            return jnp.where(is_low, left, right)

        pack_span(leaving, is_low, es, bse, bso, v * SPAN_V)
        return carry

    lax.fori_loop(0, NV, one, 0)


def chord_flux_kernel(gc, visc, rce, rco, fc, bco, bce):
    i, _ = row_ids()
    first_row = i == 0
    ec = even_chord()
    weights = [
        jnp.where(i == 0, float(0.5 * CORR_L[k]), jnp.where(i == 3, float(0.5 * CORR_R[k]), 0.0))
        for k in range(5)
    ]

    def one(v, carry):
        received = {}

        def leaving(f):
            m, q = f // 4, f % 4
            if m not in received:
                base = v * CHORD_V + m
                first, second = rce[base], rco[base]
                received[m] = (jnp.where(ec, second, first), jnp.where(ec, first, second))
            edge = open_chord(received[m][0], received[m][1], q, i)
            values = []
            for k, p in enumerate(line_points(0, f)):
                value = visc[p] * (gc[v, p] + weights[k] * edge)
                fc[v, p] = value
                values.append(value)
            left, right = traces(even_odd(values))
            return jnp.where(first_row, left, right)

        pack_chord(leaving, i, ec, bce, bco, v * CHORD_V)
        return carry

    lax.fori_loop(0, NV, one, 0)


def divergence_kernel(gn, visc, fs, fc, res, total_ref, diff_ref):
    i, j = row_ids()
    lane = lane_ids()
    is_low = j == 0
    sign_row = jnp.where(is_low, 1.0, -1.0)

    def one(v, carry):
        def normal_flux(f):
            return even_odd([visc[p] * gn[v, p] for p in line_points(2, f)])

        for f in range(NF):
            left, right = traces(normal_flux(f))
            total_ref[f], diff_ref[f] = neighbours_normal(left, right, -1.0, lane)
        for axis, ref in ((0, fc), (1, fs), (2, gn)):
            for f in range(NF):
                points = line_points(axis, f)
                if axis == 2:
                    parts = normal_flux(f)
                    total, diff = total_ref[f], diff_ref[f]
                else:
                    parts = even_odd([ref[v, p] for p in points])
                    left, right = traces(parts)
                    if axis == 0:
                        total, diff = neighbours_chord(left, right, -1.0, i)
                    else:
                        total, diff = neighbours_span(left, right, is_low, sign_row)
                for p, value in zip(points, slope(parts, total, diff)):
                    res[v, p] = value if axis == 0 else res[v, p] + value
        return carry

    lax.fori_loop(0, NV, one, 0)


def close_kernel(res, rbse, rbso, rbce, rbco, out, span_edge, chord_edge):
    i, j = row_ids()
    is_low = j == 0
    es, ec = even_span(), even_chord()
    wspan = [jnp.where(is_low, float(0.5 * CORR_L[k]), float(0.5 * CORR_R[k])) for k in range(5)]
    wchord = [
        jnp.where(i == 0, float(0.5 * CORR_L[k]), jnp.where(i == 3, float(0.5 * CORR_R[k]), 0.0))
        for k in range(5)
    ]

    def one(v, carry):
        for f in range(NF):
            base = v * SPAN_V + f // 2
            first, second = rbse[base], rbso[base]
            span_edge[f] = open_span(
                jnp.where(es, second, first), jnp.where(es, first, second), f % 2, is_low
            )
            base = v * CHORD_V + f // 4
            first, second = rbce[base], rbco[base]
            chord_edge[f] = open_chord(
                jnp.where(ec, second, first), jnp.where(ec, first, second), f % 4, i
            )
        for a in range(5):
            for b in range(5):
                for c in range(5):
                    p = 25 * a + 5 * b + c
                    out[v, p] = res[v, p] + (
                        wspan[b] * span_edge[5 * a + c] + wchord[a] * chord_edge[5 * b + c]
                    )
        return carry

    lax.fori_loop(0, NV, one, 0)


def vec(*lead):
    return jax.ShapeDtypeStruct(lead + (ROWS, LANES), jnp.float32)


def call(kernel, name, outs, args, scratch=(), alias=None, cycles=1000):
    vmem = pl.BlockSpec(memory_space=pltpu.VMEM)
    total = sum(int(np.prod(x.shape)) for x in list(outs) + list(args)) * 4
    return pl.pallas_call(
        kernel,
        out_shape=outs,
        in_specs=[vmem] * len(args),
        out_specs=[vmem] * len(outs),
        scratch_shapes=[pltpu.VMEM(s.shape, s.dtype) for s in scratch],
        input_output_aliases=alias or {},
        compiler_params=pltpu.CompilerParams(vmem_limit_bytes=VMEM_LIMIT),
        cost_estimate=pl.CostEstimate(flops=cycles * 4096, bytes_accessed=total, transcendentals=0),
        name=name,
    )(*args)


VMEM_LIMIT = 24 * 2**20


def paired(n, odd, wraps):
    route = []
    for lower in range(odd, n, 2):
        upper = lower + 1
        if upper >= n:
            if not wraps:
                continue
            upper %= n
        route += [(lower, upper), (upper, lower)]
    return route


def shards(state):
    chords, spans = lax.axis_size("chord"), lax.axis_size("span")

    def span_swap(array, odd):
        return lax.ppermute(array, "span", paired(spans, odd, True))

    def chord_swap(array, odd):
        return lax.ppermute(array, "chord", paired(chords, odd, False))

    u = state.reshape(NV, 125, ROWS, LANES)
    so, se, co, ce, eps = call(
        leave_kernel,
        "leave",
        [vec(SPAN_N + 1), vec(SPAN_N + 1), vec(CHORD_N + 1), vec(CHORD_N + 1), vec()],
        [u],
        [vec(125)],
    )
    rso = span_swap(so, 1)
    rce = chord_swap(ce, 0)
    rco = chord_swap(co, 1)
    rse = span_swap(se, 0)
    gc, gs, gn = call(
        gradient_kernel, "gradient", [vec(NV, 125)] * 3, [u], [vec(NF), vec(NF)], cycles=5000
    )
    (cor,) = call(corner_kernel, "corner", [vec(2)], [rce, rco])
    rcse = span_swap(cor, 0)
    rcso = span_swap(cor, 1)
    visc, fs, bso, bse = call(
        span_flux_kernel,
        "span_flux",
        [vec(125), vec(NV, 125), vec(SPAN_N), vec(SPAN_N)],
        [gs, eps, rcse, rcso, rse, rso, rce, rco],
        alias={0: 1},
        cycles=2000,
    )
    rbso = span_swap(bso, 1)
    fc, bco, bce = call(
        chord_flux_kernel,
        "chord_flux",
        [vec(NV, 125), vec(CHORD_N), vec(CHORD_N)],
        [gc, visc, rce, rco],
        alias={0: 0},
        cycles=2000,
    )
    rbco = chord_swap(bco, 1)
    rbce = chord_swap(bce, 0)
    rbse = span_swap(bse, 0)
    (res,) = call(
        divergence_kernel,
        "divergence",
        [vec(NV, 125)],
        [gn, visc, fs, fc],
        [vec(NF), vec(NF)],
        cycles=6000,
    )
    (out,) = call(
        close_kernel,
        "close",
        [vec(NV, 125)],
        [res, rbse, rbso, rbce, rbco],
        [vec(NF), vec(NF)],
        alias={0: 0},
        cycles=2000,
    )
    return (out.reshape(state.shape), visc.reshape(state.shape[1:]))


def solution(mesh):
    in_specs = (P(None, None, "chord", "span", None),)
    out_specs = (P(None, None, "chord", "span", None), P(None, "chord", "span", None))
    return jax.shard_map(shards, mesh=mesh, in_specs=in_specs, out_specs=out_specs, check_vma=False)
```

profile of v0, /device:TPU:8, one launch (start us, length us, event | category | flops | bytes accessed | tf_op | source)
XLA Modules:
  0.0 48.9 jit_solution(2828223589553394070)
XLA Ops:
  0.6 0.0 copy-start
  0.6 1.7 %copy-done = f32[5,125,4,2,128]{4,3,2,1,0:T(2,128)S(1)} copy-done((f32[5,125,4,2,128]{4,3,2,1,0:T(2,128)S(1)}, f32[5,125,4,2,128]{4,3,2,1,0:T(2,128)}, u32[]{:S(2)}) %copy-start) | copy-done | bytes 2560024
  2.4 0.0 copy-start.1
  2.4 1.0 %leave.1 = (f32[66,8,128]{2,1,0:T(8,128)S(1)}, f32[66,8,128]{2,1,0:T(8,128)S(1)}, f32[36,8,128]{2,1,0:T(8,128)S(1)}, f32[36,8,128]{2,1,0:T(8,128)S(1)}, f32[8,128]{1,0:T(8,128)S(1)}) custom-call(f32[5,125,8,128]{3,2,1,0:T(8,128)S(1)} %bitcast.3), custom_call_target="tpu_custom_call" | custom-call | flops 4096000 | bytes 3399680 | tf_op jit(solution)/shard_map/leave/pallas_call | solution.py:493
  3.3 0.1 collective-permute-start.4
  3.4 4.6 %collective-permute-start.5 = (f32[66,8,128]{2,1,0:T(8,128)S(1)}, f32[66,8,128]{2,1,0:T(8,128)S(1)}, u32[]{:S(2)}, u32[]{:S(2)}) collective-permute-start(f32[66,8,128]{2,1,0:T(8,128)S(1)} %get-tuple-element.23), channel_id=1, source_target_pairs={{1,2},{2,1},{3,4},{4,3},{5,6},{6,5},{7,8},{8,7},{9,10},{10,9},{11,... | collective-permute-start | bytes 811016 | tf_op jit(solution)/shard_map/ppermute | solution.py:525
  8.0 1.9 %collective-permute-start = (f32[36,8,128]{2,1,0:T(8,128)S(1)}, f32[36,8,128]{2,1,0:T(8,128)S(1)}, u32[]{:S(2)}, u32[]{:S(2)}) collective-permute-start(f32[36,8,128]{2,1,0:T(8,128)S(1)} %get-tuple-element.20), channel_id=1, source_target_pairs={{0,16},{16,0},{32,48},{48,32},{64,80},{80,64},{96,112},{112,96},{1... | collective-permute-start | bytes 442376 | tf_op jit(solution)/shard_map/ppermute | solution.py:528
  10.0 5.2 %collective-permute-start.1 = (f32[36,8,128]{2,1,0:T(8,128)S(1)}, f32[36,8,128]{2,1,0:T(8,128)S(1)}, u32[]{:S(2)}, u32[]{:S(2)}) collective-permute-start(f32[36,8,128]{2,1,0:T(8,128)S(1)} %get-tuple-element.21), channel_id=1, source_target_pairs={{16,32},{32,16},{48,64},{64,48},{80,96},{96,80},{17,33},{33,17},{4... | collective-permute-start | bytes 442376 | tf_op jit(solution)/shard_map/ppermute | solution.py:528
  15.2 0.0 collective-permute-done.rce
  15.2 5.4 %collective-permute-done.1.rco = f32[36,8,128]{2,1,0:T(8,128)S(1)} collective-permute-done((f32[36,8,128]{2,1,0:T(8,128)S(1)}, f32[36,8,128]{2,1,0:T(8,128)S(1)}, u32[]{:S(2)}, u32[]{:S(2)}) %collective-permute-start.1) | collective-permute-done | bytes 147488 | tf_op jit(solution)/shard_map/ppermute | solution.py:528
  20.6 0.0 collective-permute-start.3
  20.6 0.4 collective-permute-start.2
  21.0 0.0 copy-done.1
  21.0 2.7 %gradient.1 = (f32[5,125,8,128]{3,2,1,0:T(8,128)S(1)}, f32[5,125,8,128]{3,2,1,0:T(8,128)S(1)}, f32[5,125,8,128]{3,2,1,0:T(8,128)S(1)}) custom-call(f32[5,125,8,128]{3,2,1,0:T(8,128)S(1)} %bitcast.4), custom_call_target="tpu_custom_call" | custom-call | flops 20480000 | bytes 10240000 | tf_op jit(solution)/shard_map/gradient/pallas_call | solution.py:493
  23.7 3.5 %collective-permute-done.3.rcso = f32[2,8,128]{2,1,0:T(8,128)S(1)} collective-permute-done((f32[2,8,128]{2,1,0:T(8,128)S(1)}, f32[2,8,128]{2,1,0:T(8,128)S(1)}, u32[]{:S(2)}, u32[]{:S(2)}) %collective-permute-start.3) | collective-permute-done | bytes 8224 | tf_op jit(solution)/shard_map/ppermute | solution.py:525
  27.3 0.0 collective-permute-done.2.rcse
  27.3 0.0 collective-permute-done.4.rse
  27.3 0.0 collective-permute-done.5.rso
  27.3 3.1 %span_flux.1 = (f32[125,8,128]{2,1,0:T(8,128)}, f32[5,125,8,128]{3,2,1,0:T(8,128)S(1)}, f32[65,8,128]{2,1,0:T(8,128)S(1)}, f32[65,8,128]{2,1,0:T(8,128)S(1)}) custom-call(f32[5,125,8,128]{3,2,1,0:T(8,128)S(1)} %get-tuple-element.18.gs, f32[8,128]{1,0:T(8,128)S(1)} %get-tuple-element.19.eps, ...), custom_call_target="tpu_custom_call", output_to_operand_aliasing={{1}: (0, {})} | custom-call | flops 8192000 | bytes 7020544 | tf_op jit(solution)/shard_map/span_flux/pallas_call | solution.py:493
  30.4 0.0 collective-permute-start.6
  30.4 1.9 %collective-permute-start.7 = (f32[65,8,128]{2,1,0:T(8,128)S(1)}, f32[65,8,128]{2,1,0:T(8,128)S(1)}, u32[]{:S(2)}, u32[]{:S(2)}) collective-permute-start(f32[65,8,128]{2,1,0:T(8,128)S(1)} %get-tuple-element.29), channel_id=1, source_target_pairs={{1,2},{2,1},{3,4},{4,3},{5,6},{6,5},{7,8},{8,7},{9,10},{10,9},{11,... | collective-permute-start | bytes 798728 | tf_op jit(solution)/shard_map/ppermute | solution.py:525
  32.3 0.0 copy-start.2
  32.3 1.0 %copy-done.2 = f32[125,8,128]{2,1,0:T(8,128)S(1)} copy-done((f32[125,8,128]{2,1,0:T(8,128)S(1)}, f32[125,8,128]{2,1,0:T(8,128)}, u32[]{:S(2)}) %copy-start.2) | copy-done | bytes 512024
  33.3 2.7 %chord_flux.1 = (f32[5,125,8,128]{3,2,1,0:T(8,128)S(1)}, f32[35,8,128]{2,1,0:T(8,128)S(1)}, f32[35,8,128]{2,1,0:T(8,128)S(1)}) custom-call(f32[5,125,8,128]{3,2,1,0:T(8,128)S(1)} %get-tuple-element.26.gc, f32[125,8,128]{2,1,0:T(8,128)S(1)} %copy-done.2, f32[36,8,128]{2,1,0:T(8,128)S(1)} %collective-permute-done.rce, ...), custom_call_target="tpu_custom_call", output_to_operand_aliasing={{0}: (0, {})} | custom-call | flops 8192000 | bytes 6213632 | tf_op jit(solution)/shard_map/chord_flux/pallas_call | solution.py:493
  36.0 0.1 collective-permute-start.8
  36.1 3.7 %collective-permute-start.9 = (f32[35,8,128]{2,1,0:T(8,128)S(1)}, f32[35,8,128]{2,1,0:T(8,128)S(1)}, u32[]{:S(2)}, u32[]{:S(2)}) collective-permute-start(f32[35,8,128]{2,1,0:T(8,128)S(1)} %get-tuple-element.31), channel_id=1, source_target_pairs={{16,32},{32,16},{48,64},{64,48},{80,96},{96,80},{17,33},{33,17},{4... | collective-permute-start | bytes 430088 | tf_op jit(solution)/shard_map/ppermute | solution.py:528
  39.9 4.8 %divergence.1.res = f32[5,125,8,128]{3,2,1,0:T(8,128)} custom-call(f32[5,125,8,128]{3,2,1,0:T(8,128)S(1)} %get-tuple-element.17.gn, f32[125,8,128]{2,1,0:T(8,128)S(1)} %copy-done.2, f32[5,125,8,128]{3,2,1,0:T(8,128)S(1)} %get-tuple-element.25.fs, f32[5,125,8,128]{3,2,1,0:T(8,128)S(1)} %get-tuple-element.27.fc), custom_call_target="tpu_custom_call" | custom-call | flops 24576000 | bytes 10752000 | tf_op jit(solution)/shard_map/divergence/pallas_call | solution.py:493
  44.7 0.0 collective-permute-done.8.rbce
  44.7 0.5 %collective-permute-done.9.rbco = f32[35,8,128]{2,1,0:T(8,128)S(1)} collective-permute-done((f32[35,8,128]{2,1,0:T(8,128)S(1)}, f32[35,8,128]{2,1,0:T(8,128)S(1)}, u32[]{:S(2)}, u32[]{:S(2)}) %collective-permute-start.9) | collective-permute-done | bytes 143392 | tf_op jit(solution)/shard_map/ppermute | solution.py:528
  45.2 0.0 collective-permute-done.6.rbse
  45.2 0.0 collective-permute-done.7.rbso
  45.2 3.7 %close.1 = f32[5,125,8,128]{3,2,1,0:T(8,128)} custom-call(f32[5,125,8,128]{3,2,1,0:T(8,128)} %divergence.1.res, f32[65,8,128]{2,1,0:T(8,128)S(1)} %collective-permute-done.6.rbse, f32[65,8,128]{2,1,0:T(8,128)S(1)} %collective-permute-done.7.rbso, f32[35,8,128]{2,1,0:T(8,128)S(1)} %collective-permute-done.8.rbce, ...), custom_call_target="tpu_custom_call", output_to_operand_aliasing={{}: (0, {})} | custom-call | flops 8192000 | bytes 5939200 | tf_op jit(solution)/shard_map/close/pallas_call | solution.py:493
  (1 shorter events, 0.0 us)
Async XLA Ops:
  0.6 1.7 %copy-start = (f32[5,125,4,2,128]{4,3,2,1,0:T(2,128)S(1)}, f32[5,125,4,2,128]{4,3,2,1,0:T(2,128)}, u32[]{:S(2)}) copy-start(f32[5,125,4,2,128]{4,3,2,1,0:T(2,128)} %param.1) | copy-start | bytes 7680004
  2.4 18.7 %copy-start.1 = (f32[5,125,4,2,128]{4,3,2,1,0:T(2,128)S(1)}, f32[5,125,4,2,128]{4,3,2,1,0:T(2,128)}, u32[]{:S(2)}) copy-start(f32[5,125,4,2,128]{4,3,2,1,0:T(2,128)} %param.1) | copy-start | bytes 7680004
  3.3 23.9 %collective-permute-start.4 = (f32[66,8,128]{2,1,0:T(8,128)S(1)}, f32[66,8,128]{2,1,0:T(8,128)S(1)}, u32[]{:S(2)}, u32[]{:S(2)}) collective-permute-start(f32[66,8,128]{2,1,0:T(8,128)S(1)} %get-tuple-element.22), channel_id=1, source_target_pairs={{0,1},{1,0},{2,3},{3,2},{4,5},{5,4},{6,7},{7,6},{8,9},{9,8},{10,11... | collective-permute-start | bytes 811016 | tf_op jit(solution)/shard_map/ppermute | solution.py:525
  3.4 23.8 %collective-permute-start.5 = (f32[66,8,128]{2,1,0:T(8,128)S(1)}, f32[66,8,128]{2,1,0:T(8,128)S(1)}, u32[]{:S(2)}, u32[]{:S(2)}) collective-permute-start(f32[66,8,128]{2,1,0:T(8,128)S(1)} %get-tuple-element.23), channel_id=1, source_target_pairs={{1,2},{2,1},{3,4},{4,3},{5,6},{6,5},{7,8},{8,7},{9,10},{10,9},{11,... | collective-permute-start | bytes 811016 | tf_op jit(solution)/shard_map/ppermute | solution.py:525
  8.0 7.1 %collective-permute-start = (f32[36,8,128]{2,1,0:T(8,128)S(1)}, f32[36,8,128]{2,1,0:T(8,128)S(1)}, u32[]{:S(2)}, u32[]{:S(2)}) collective-permute-start(f32[36,8,128]{2,1,0:T(8,128)S(1)} %get-tuple-element.20), channel_id=1, source_target_pairs={{0,16},{16,0},{32,48},{48,32},{64,80},{80,64},{96,112},{112,96},{1... | collective-permute-start | bytes 442376 | tf_op jit(solution)/shard_map/ppermute | solution.py:528
  10.0 10.6 %collective-permute-start.1 = (f32[36,8,128]{2,1,0:T(8,128)S(1)}, f32[36,8,128]{2,1,0:T(8,128)S(1)}, u32[]{:S(2)}, u32[]{:S(2)}) collective-permute-start(f32[36,8,128]{2,1,0:T(8,128)S(1)} %get-tuple-element.21), channel_id=1, source_target_pairs={{16,32},{32,16},{48,64},{64,48},{80,96},{96,80},{17,33},{33,17},{4... | collective-permute-start | bytes 442376 | tf_op jit(solution)/shard_map/ppermute | solution.py:528
  20.6 6.7 %collective-permute-start.3 = (f32[2,8,128]{2,1,0:T(8,128)S(1)}, f32[2,8,128]{2,1,0:T(8,128)S(1)}, u32[]{:S(2)}, u32[]{:S(2)}) collective-permute-start(f32[2,8,128]{2,1,0:T(8,128)S(1)} %corner.1), channel_id=1, source_target_pairs={{1,2},{2,1},{3,4},{4,3},{5,6},{6,5},{7,8},{8,7},{9,10},{10,9},{11,... | collective-permute-start | bytes 24584 | tf_op jit(solution)/shard_map/ppermute | solution.py:525
  20.6 6.7 %collective-permute-start.2 = (f32[2,8,128]{2,1,0:T(8,128)S(1)}, f32[2,8,128]{2,1,0:T(8,128)S(1)}, u32[]{:S(2)}, u32[]{:S(2)}) collective-permute-start(f32[2,8,128]{2,1,0:T(8,128)S(1)} %corner.1), channel_id=1, source_target_pairs={{0,1},{1,0},{2,3},{3,2},{4,5},{5,4},{6,7},{7,6},{8,9},{9,8},{10,11... | collective-permute-start | bytes 24584 | tf_op jit(solution)/shard_map/ppermute | solution.py:525
  30.4 14.8 %collective-permute-start.6 = (f32[65,8,128]{2,1,0:T(8,128)S(1)}, f32[65,8,128]{2,1,0:T(8,128)S(1)}, u32[]{:S(2)}, u32[]{:S(2)}) collective-permute-start(f32[65,8,128]{2,1,0:T(8,128)S(1)} %get-tuple-element.28), channel_id=1, source_target_pairs={{0,1},{1,0},{2,3},{3,2},{4,5},{5,4},{6,7},{7,6},{8,9},{9,8},{10,11... | collective-permute-start | bytes 798728 | tf_op jit(solution)/shard_map/ppermute | solution.py:525
  30.4 14.8 %collective-permute-start.7 = (f32[65,8,128]{2,1,0:T(8,128)S(1)}, f32[65,8,128]{2,1,0:T(8,128)S(1)}, u32[]{:S(2)}, u32[]{:S(2)}) collective-permute-start(f32[65,8,128]{2,1,0:T(8,128)S(1)} %get-tuple-element.29), channel_id=1, source_target_pairs={{1,2},{2,1},{3,4},{4,3},{5,6},{6,5},{7,8},{8,7},{9,10},{10,9},{11,... | collective-permute-start | bytes 798728 | tf_op jit(solution)/shard_map/ppermute | solution.py:525
  32.3 1.0 %copy-start.2 = (f32[125,8,128]{2,1,0:T(8,128)S(1)}, f32[125,8,128]{2,1,0:T(8,128)}, u32[]{:S(2)}) copy-start(f32[125,8,128]{2,1,0:T(8,128)} %get-tuple-element.24.visc) | copy-start | bytes 1536004
  36.0 8.7 %collective-permute-start.8 = (f32[35,8,128]{2,1,0:T(8,128)S(1)}, f32[35,8,128]{2,1,0:T(8,128)S(1)}, u32[]{:S(2)}, u32[]{:S(2)}) collective-permute-start(f32[35,8,128]{2,1,0:T(8,128)S(1)} %get-tuple-element.30), channel_id=1, source_target_pairs={{0,16},{16,0},{32,48},{48,32},{64,80},{80,64},{96,112},{112,96},{1... | collective-permute-start | bytes 430088 | tf_op jit(solution)/shard_map/ppermute | solution.py:528
  36.1 9.1 %collective-permute-start.9 = (f32[35,8,128]{2,1,0:T(8,128)S(1)}, f32[35,8,128]{2,1,0:T(8,128)S(1)}, u32[]{:S(2)}, u32[]{:S(2)}) collective-permute-start(f32[35,8,128]{2,1,0:T(8,128)S(1)} %get-tuple-element.31), channel_id=1, source_target_pairs={{16,32},{32,16},{48,64},{64,48},{80,96},{96,80},{17,33},{33,17},{4... | collective-permute-start | bytes 430088 | tf_op jit(solution)/shard_map/ppermute | solution.py:528
where the time goes:
time: 49.1 us; the launch traced here: 48.9 us
  Pallas kernels  18 us (37%)
  starting transfers between devices  18 us (37%)
  waiting for transfers between devices  9.46 us (19%)
  local copies, waits for them, and re-layouts  2.76 us (6%)
  between operations  0.7 us (1%)
    pallas_call x7, Pallas kernels, call(): pl.pallas_call(kernel, out_shape=outs, in_specs=[vmem] * len(args), out_s...  18 us
    ppermute x4, starting transfers between devices, chord_swap(): return lax.ppermute(array, 'chord', paired(chords, odd, False))  11 us
    ppermute x6, starting transfers between devices, span_swap(): return lax.ppermute(array, 'span', paired(spans, odd, True))  7.05 us
    ppermute x4, waiting for transfers between devices, chord_swap(): return lax.ppermute(array, 'chord', paired(chords, odd, False))  5.92 us
    ppermute x6, waiting for transfers between devices, span_swap(): return lax.ppermute(array, 'span', paired(spans, odd, True))  3.54 us
    unnamed x6, local copies, waits for them, and re-layouts  2.76 us
  transfers between devices with their start and end apart: 10, of which 3 were waited for; matrix products, arithmetic and copies ran while one was open for 0% of the time, Pallas kernels for 21%

commit v1 on v0

--- a/solution.py
+++ b/solution.py
@@ -1,4 +1,3 @@
-import functools
 import math
 
 import jax
@@ -8,6 +7,7 @@
 from jax.experimental import pallas as pl
 from jax.experimental.pallas import tpu as pltpu
 from jax.sharding import PartitionSpec as P
+
 
 EPS_SCALE = 0.01
 SENSOR_CENTRE = -3.0
@@ -153,6 +153,11 @@
     return jnp.full((ROWS, LANES), flag.astype(jnp.int32), jnp.int32) > 0
 
 
+def chord_ends():
+    at = lax.axis_index("chord")
+    return (splat_flag(at == 0), splat_flag(at == lax.axis_size("chord") - 1))
+
+
 def even_span():
     return splat_flag(lax.axis_index("span") % 2 == 0)
 
@@ -196,26 +201,64 @@
     return jnp.where(i == 0, up_rows(below, -2 * q), up_rows(above, 6 - 2 * q))
 
 
-def leave_kernel(state, so, se, co, ce, eps_ref, work):
-    i, j = row_ids()
-    is_low, first_row = j == 0, i == 0
-    es, ec = even_span(), even_chord()
-
-    def one(v, carry):
-        def leaving(axis, mask, f):
-            left, right = traces(even_odd([state[v, p] for p in line_points(axis, f)]))
-            return jnp.where(mask, left, right)
-
-        pack_span(functools.partial(leaving, 1, is_low), is_low, es, se, so, v * SPAN_V)
-        pack_chord(functools.partial(leaving, 0, first_row), i, ec, ce, co, v * CHORD_V)
+def sided(even, first, second):
+    return (jnp.where(even, second, first), jnp.where(even, first, second))
+
+
+def leave_span_kernel(source, so, se, eps_ref, state, work, sems):
+    reads = [pltpu.make_async_copy(source.at[v], state.at[v], sems.at[v]) for v in range(NV)]
+    for read in reads:
+        read.start()
+    _, j = row_ids()
+    is_low = j == 0
+    es = even_span()
+
+    def one(v, carry):
+        def leaving(f):
+            left, right = traces(even_odd([state[v, p] for p in line_points(1, f)]))
+            return jnp.where(is_low, left, right)
+
+        pack_span(leaving, is_low, es, se, so, v * SPAN_V)
+        return carry
+
+    reads[0].wait()
+    eps = sensor(state, work)
+    eps_ref[...] = eps
+    se[SPAN_N] = eps
+    one(0, 0)
+
+    def later(v, carry):
+        pltpu.make_async_copy(source.at[v], state.at[v], sems.at[v]).wait()
+        return one(v, carry)
+
+    lax.fori_loop(1, NV, later, 0)
+
+
+def leave_chord_kernel(state, eps, rkso, rse, co, ce):
+    i, _ = row_ids()
+    first_row = i == 0
+    ec = even_chord()
+
+    def one(v, carry):
+        def leaving(f):
+            left, right = traces(even_odd([state[v, p] for p in line_points(0, f)]))
+            return jnp.where(first_row, left, right)
+
+        pack_chord(leaving, i, ec, ce, co, v * CHORD_V)
         return carry
 
     lax.fori_loop(0, NV, one, 0)
+    before, after = sided(even_span(), rse[SPAN_N], rkso[...])
+    for ref in (co, ce):
+        ref[CHORD_N], ref[CHORD_N + 1], ref[CHORD_N + 2] = eps[...], before, after
+
+
+def sensor(state, work):
     for axis in range(2):
-        source = state.at[0] if axis == 0 else work
+        origin = state.at[0] if axis == 0 else work
         for f in range(NF):
             points = line_points(axis, f)
-            for p, value in zip(points, modal_line([source[p] for p in points])):
+            for p, value in zip(points, modal_line([origin[p] for p in points])):
                 work[p] = value
     low_sums, high_sums = [], []
     for f in range(NF):
@@ -244,16 +287,7 @@
     level = jnp.log(jnp.maximum(high_part / total, RATIO_FLOOR)) * (1.0 / math.log(10.0))
     ramp = jnp.clip((level - SENSOR_CENTRE) / SENSOR_WIDTH, -1.0, 1.0)
     eps = EPS_SCALE * 0.5 * (1.0 + jnp.sin(0.5 * math.pi * ramp))
-    eps_ref[...] = eps
-    for ref, at in ((so, SPAN_N), (se, SPAN_N), (co, CHORD_N), (ce, CHORD_N)):
-        ref[at] = eps
-
-
-def corner_kernel(rce, rco, cor):
-    ec = even_chord()
-    first, second = rce[CHORD_N], rco[CHORD_N]
-    cor[0] = jnp.where(ec, second, first)
-    cor[1] = jnp.where(ec, first, second)
+    return eps
 
 
 def neighbours_chord(left, right, sign, i):
@@ -306,7 +340,7 @@
     lax.fori_loop(0, NV, one, 0)
 
 
-def viscosity_into(visc, own, below, above, before, after, cb, ca):
+def viscosity_into(visc, own, behind, ahead):
     i, j = row_ids()
     lane = lane_ids()
     is_low = j == 0
@@ -316,9 +350,7 @@
         over = up_rows(jnp.where(i == 0, high, mid), -2)
         return (jnp.maximum(mid, under), jnp.maximum(mid, over))
 
-    mids = chord_pair(own, below, above)
-    befores = chord_pair(before, cb[0], cb[1])
-    afters = chord_pair(after, ca[0], ca[1])
+    mids, befores, afters = (chord_pair(own[n], behind[n], ahead[n]) for n in range(3))
     corners = {}
     for x in range(2):
         mid, low, high = mids[x], befores[x], afters[x]
@@ -344,21 +376,12 @@
                 visc[25 * a + 5 * b + c] = mul(halves[c][0], low) + mul(halves[c][1], high)
 
 
-def span_flux_kernel(gs, eps, rcse, rcso, rse, rso, rce, rco, visc, fs, bso, bse):
-    i, j = row_ids()
+def span_flux_kernel(gs, visc, rse, rso, fs, bso, bse):
+    _, j = row_ids()
     is_low = j == 0
     es, ec = even_span(), even_chord()
 
-    def sides(even, first, second):
-        return (jnp.where(even, second, first), jnp.where(even, first, second))
-
-    below, above = sides(ec, rce[CHORD_N], rco[CHORD_N])
-    before, after = sides(es, rse[SPAN_N], rso[SPAN_N])
-    low = [sides(es, rcse[n], rcso[n]) for n in range(2)]
-    viscosity_into(
-        visc, eps[...], below, above, before, after, (low[0][0], low[1][0]), (low[0][1], low[1][1])
-    )
-    weights = [jnp.where(is_low, float(0.5 * CORR_L[k]), float(0.5 * CORR_R[k])) for k in range(5)]
+    weights = span_weights(is_low)
 
     def one(v, carry):
         received = {}
@@ -367,7 +390,7 @@
             m, q = f // 2, f % 2
             if m not in received:
                 base = v * SPAN_V + m
-                received[m] = sides(es, rse[base], rso[base])
+                received[m] = sided(es, rse[base], rso[base])
             edge = open_span(received[m][0], received[m][1], q, is_low)
             values = []
             for k, p in enumerate(line_points(1, f)):
@@ -383,14 +406,19 @@
     lax.fori_loop(0, NV, one, 0)
 
 
-def chord_flux_kernel(gc, visc, rce, rco, fc, bco, bce):
+def chord_flux_kernel(gc, eps, rkso, rse, rce, rco, visc, fc, bco, bce):
     i, _ = row_ids()
     first_row = i == 0
-    ec = even_chord()
-    weights = [
-        jnp.where(i == 0, float(0.5 * CORR_L[k]), jnp.where(i == 3, float(0.5 * CORR_R[k]), 0.0))
-        for k in range(5)
-    ]
+    es, ec = even_span(), even_chord()
+    before, after = sided(es, rse[SPAN_N], rkso[...])
+    first, last = chord_ends()
+    low, high = [], []
+    for n in range(3):
+        behind, ahead = sided(ec, rce[CHORD_N + n], rco[CHORD_N + n])
+        low.append(jnp.where(first, 0.0, behind))
+        high.append(jnp.where(last, 0.0, ahead))
+    viscosity_into(visc, (eps[...], before, after), low, high)
+    weights = chord_weights(i)
 
     def one(v, carry):
         received = {}
@@ -416,7 +444,9 @@
     lax.fori_loop(0, NV, one, 0)
 
 
-def divergence_kernel(gn, visc, fs, fc, res, total_ref, diff_ref):
+def divergence_kernel(gn, visc, fs, fc, res, visc_out, total_ref, diff_ref, sem):
+    write = pltpu.make_async_copy(visc, visc_out, sem)
+    write.start()
     i, j = row_ids()
     lane = lane_ids()
     is_low = j == 0
@@ -447,63 +477,92 @@
         return carry
 
     lax.fori_loop(0, NV, one, 0)
-
-
-def close_kernel(res, rbse, rbso, rbce, rbco, out, span_edge, chord_edge):
-    i, j = row_ids()
+    write.wait()
+
+
+def close_chord_kernel(res, rbce, rbco, out, edge):
+    i, _ = row_ids()
+    ec = even_chord()
+    weights = chord_weights(i)
+
+    def one(v, carry):
+        for m in range(CHORD_V):
+            first, second = rbce[v * CHORD_V + m], rbco[v * CHORD_V + m]
+            behind, ahead = jnp.where(ec, second, first), jnp.where(ec, first, second)
+            for f in range(4 * m, min(4 * m + 4, NF)):
+                edge[f] = open_chord(behind, ahead, f % 4, i)
+        for f in range(NF):
+            for k, p in enumerate(line_points(0, f)):
+                out[v, p] = res[v, p] + weights[k] * edge[f]
+        return carry
+
+    lax.fori_loop(0, NV, one, 0)
+
+
+def close_span_kernel(res, rbse, rbso, final, edge, out, sems):
+    _, j = row_ids()
     is_low = j == 0
-    es, ec = even_span(), even_chord()
-    wspan = [jnp.where(is_low, float(0.5 * CORR_L[k]), float(0.5 * CORR_R[k])) for k in range(5)]
-    wchord = [
-        jnp.where(i == 0, float(0.5 * CORR_L[k]), jnp.where(i == 3, float(0.5 * CORR_R[k]), 0.0))
+    es = even_span()
+    weights = span_weights(is_low)
+
+    def send(v):
+        return pltpu.make_async_copy(out.at[v], final.at[v], sems.at[v])
+
+    def one(v, carry):
+        for m in range(SPAN_V):
+            first, second = rbse[v * SPAN_V + m], rbso[v * SPAN_V + m]
+            behind, ahead = jnp.where(es, second, first), jnp.where(es, first, second)
+            for f in range(2 * m, min(2 * m + 2, NF)):
+                edge[f] = open_span(behind, ahead, f % 2, is_low)
+        for f in range(NF):
+            for k, p in enumerate(line_points(1, f)):
+                out[v, p] = res[v, p] + weights[k] * edge[f]
+
+        @pl.when(v > 0)
+        def _():
+            send(v - 1).start()
+
+        return carry
+
+    lax.fori_loop(0, NV, one, 0)
+    send(NV - 1).start()
+    for v in range(NV):
+        send(v).wait()
+
+
+def span_weights(is_low):
+    return [jnp.where(is_low, float(0.5 * CORR_L[k]), float(0.5 * CORR_R[k])) for k in range(5)]
+
+
+def chord_weights(i):
+    first, last = chord_ends()
+    low, high = jnp.logical_and(i == 0, ~first), jnp.logical_and(i == 3, ~last)
+    return [
+        jnp.where(low, float(0.5 * CORR_L[k]), jnp.where(high, float(0.5 * CORR_R[k]), 0.0))
         for k in range(5)
     ]
 
-    def one(v, carry):
-        for f in range(NF):
-            base = v * SPAN_V + f // 2
-            first, second = rbse[base], rbso[base]
-            span_edge[f] = open_span(
-                jnp.where(es, second, first), jnp.where(es, first, second), f % 2, is_low
-            )
-            base = v * CHORD_V + f // 4
-            first, second = rbce[base], rbco[base]
-            chord_edge[f] = open_chord(
-                jnp.where(ec, second, first), jnp.where(ec, first, second), f % 4, i
-            )
-        for a in range(5):
-            for b in range(5):
-                for c in range(5):
-                    p = 25 * a + 5 * b + c
-                    out[v, p] = res[v, p] + (
-                        wspan[b] * span_edge[5 * a + c] + wchord[a] * chord_edge[5 * b + c]
-                    )
-        return carry
-
-    lax.fori_loop(0, NV, one, 0)
+
+def held(*lead):
+    return pltpu.VMEM(lead + (ROWS, LANES), jnp.float32)
 
 
 def vec(*lead):
     return jax.ShapeDtypeStruct(lead + (ROWS, LANES), jnp.float32)
 
 
-def call(kernel, name, outs, args, scratch=(), alias=None, cycles=1000):
-    vmem = pl.BlockSpec(memory_space=pltpu.VMEM)
+def call(kernel, outs, args, scratch=(), cycles=1000, far_in=(), far_out=(), grant=24 * 2**20):
+    vmem, hbm = (pl.BlockSpec(memory_space=m) for m in (pltpu.VMEM, pltpu.HBM))
     total = sum(int(np.prod(x.shape)) for x in list(outs) + list(args)) * 4
     return pl.pallas_call(
         kernel,
         out_shape=outs,
-        in_specs=[vmem] * len(args),
-        out_specs=[vmem] * len(outs),
-        scratch_shapes=[pltpu.VMEM(s.shape, s.dtype) for s in scratch],
-        input_output_aliases=alias or {},
-        compiler_params=pltpu.CompilerParams(vmem_limit_bytes=VMEM_LIMIT),
+        in_specs=[hbm if n in far_in else vmem for n in range(len(args))],
+        out_specs=[hbm if n in far_out else vmem for n in range(len(outs))],
+        scratch_shapes=list(scratch),
+        compiler_params=pltpu.CompilerParams(vmem_limit_bytes=grant),
         cost_estimate=pl.CostEstimate(flops=cycles * 4096, bytes_accessed=total, transcendentals=0),
-        name=name,
     )(*args)
-
-
-VMEM_LIMIT = 24 * 2**20
 
 
 def paired(n, odd, wraps):
@@ -525,67 +584,71 @@
         return lax.ppermute(array, "span", paired(spans, odd, True))
 
     def chord_swap(array, odd):
-        return lax.ppermute(array, "chord", paired(chords, odd, False))
-
+        route = [
+            (a * spans + c, b * spans + c) for a, b in paired(chords, odd, False) for c in range(spans)
+        ]
+        if odd:
+            route += [
+                (a * spans + c, a * spans + (c ^ 1)) for a in (0, chords - 1) for c in range(spans)
+            ]
+        return lax.ppermute(array, ("chord", "span"), route)
+
+    dma = pltpu.SemaphoreType.DMA
     u = state.reshape(NV, 125, ROWS, LANES)
-    so, se, co, ce, eps = call(
-        leave_kernel,
-        "leave",
-        [vec(SPAN_N + 1), vec(SPAN_N + 1), vec(CHORD_N + 1), vec(CHORD_N + 1), vec()],
-        [u],
-        [vec(125)],
-    )
+    so, se, eps, near = call(
+        leave_span_kernel,
+        [vec(SPAN_N), vec(SPAN_N + 1), vec(), vec(NV, 125)],
+        [pltpu.with_memory_space_constraint(u, pltpu.HBM)],
+        [held(125), dma((NV,))],
+        far_in=(0,),
+    )
+    rkso = span_swap(eps, 1)
+    rse = span_swap(se, 0)
     rso = span_swap(so, 1)
+    co, ce = call(leave_chord_kernel, [vec(CHORD_N + 3), vec(CHORD_N + 3)], [near, eps, rkso, rse])
+    rco = chord_swap(co, 1)
     rce = chord_swap(ce, 0)
-    rco = chord_swap(co, 1)
-    rse = span_swap(se, 0)
     gc, gs, gn = call(
-        gradient_kernel, "gradient", [vec(NV, 125)] * 3, [u], [vec(NF), vec(NF)], cycles=5000
-    )
-    (cor,) = call(corner_kernel, "corner", [vec(2)], [rce, rco])
-    rcse = span_swap(cor, 0)
-    rcso = span_swap(cor, 1)
-    visc, fs, bso, bse = call(
+        gradient_kernel, [vec(NV, 125)] * 3, [near], [held(NF), held(NF)], cycles=5000
+    )
+    visc, fc, bco, bce = call(
+        chord_flux_kernel,
+        [vec(125), vec(NV, 125), vec(CHORD_N), vec(CHORD_N)],
+        [gc, eps, rkso, rse, rce, rco],
+        cycles=2000,
+    )
+    rbco = chord_swap(bco, 1)
+    fs, bso, bse = call(
         span_flux_kernel,
-        "span_flux",
-        [vec(125), vec(NV, 125), vec(SPAN_N), vec(SPAN_N)],
-        [gs, eps, rcse, rcso, rse, rso, rce, rco],
-        alias={0: 1},
+        [vec(NV, 125), vec(SPAN_N), vec(SPAN_N)],
+        [gs, visc, rse, rso],
         cycles=2000,
     )
     rbso = span_swap(bso, 1)
-    fc, bco, bce = call(
-        chord_flux_kernel,
-        "chord_flux",
-        [vec(NV, 125), vec(CHORD_N), vec(CHORD_N)],
-        [gc, visc, rce, rco],
-        alias={0: 0},
+    rbse = span_swap(bse, 0)
+    rbce = chord_swap(bce, 0)
+    res, visc_out = call(
+        divergence_kernel,
+        [vec(NV, 125), vec(125)],
+        [gn, visc, fs, fc],
+        [held(NF), held(NF), dma(())],
+        cycles=6000,
+        far_out=(1,),
+    )
+    (res,) = call(close_chord_kernel, [vec(NV, 125)], [res, rbce, rbco], [held(NF)], cycles=1000)
+    (out,) = call(
+        close_span_kernel,
+        [vec(NV, 125)],
+        [res, rbse, rbso],
+        [held(NF), held(NV, 125), dma((NV,))],
         cycles=2000,
-    )
-    rbco = chord_swap(bco, 1)
-    rbce = chord_swap(bce, 0)
-    rbse = span_swap(bse, 0)
-    (res,) = call(
-        divergence_kernel,
-        "divergence",
-        [vec(NV, 125)],
-        [gn, visc, fs, fc],
-        [vec(NF), vec(NF)],
-        cycles=6000,
-    )
-    (out,) = call(
-        close_kernel,
-        "close",
-        [vec(NV, 125)],
-        [res, rbse, rbso, rbce, rbco],
-        [vec(NF), vec(NF)],
-        alias={0: 0},
-        cycles=2000,
-    )
-    return (out.reshape(state.shape), visc.reshape(state.shape[1:]))
+        far_out=(0,),
+    )
+    return (out.reshape(state.shape), visc_out.reshape(state.shape[1:]))
 
 
 def solution(mesh):
     in_specs = (P(None, None, "chord", "span", None),)
     out_specs = (P(None, None, "chord", "span", None), P(None, "chord", "span", None))
+
     return jax.shard_map(shards, mesh=mesh, in_specs=in_specs, out_specs=out_specs, check_vma=False)

time: 49.1 us -> 41.9 us (0.85)
  the two profiles are of different devices: /device:TPU:8 before, /device:TPU:15 now
where the time goes in v1:
time: 41.9 us; the launch traced here: 41.8 us
  waiting for transfers between devices  15.4 us (37%)
  starting transfers between devices  14 us (33%)
  Pallas kernels  11.6 us (28%)
  between operations  0.72 us (2%)
    pallas_call x8, Pallas kernels, call(): pl.pallas_call(kernel, out_shape=outs, in_specs=[hbm if n in far_in else...  11.6 us
    ppermute x4, waiting for transfers between devices, chord_swap(): return lax.ppermute(array, ('chord', 'span'), route)  8.32 us
    ppermute x5, starting transfers between devices, span_swap(): return lax.ppermute(array, 'span', paired(spans, odd, True))  7.14 us
    ppermute x5, waiting for transfers between devices, span_swap(): return lax.ppermute(array, 'span', paired(spans, odd, True))  7.05 us
    ppermute x4, starting transfers between devices, chord_swap(): return lax.ppermute(array, ('chord', 'span'), route)  6.88 us
  transfers between devices with their start and end apart: 9, of which 3 were waited for; matrix products, arithmetic and copies ran while one was open for 0% of the time, Pallas kernels for 18%

profile of v1, /device:TPU:15, one launch (start us, length us, event | category | flops | bytes accessed | tf_op | source)
XLA Modules:
  0.0 41.8 jit_solution(13789301339195354824)
XLA Ops:
  0.6 1.8 %shard_map.30 = (f32[65,8,128]{2,1,0:T(8,128)S(1)}, f32[66,8,128]{2,1,0:T(8,128)S(1)}, f32[8,128]{1,0:T(8,128)S(1)}, f32[5,125,8,128]{3,2,1,0:T(8,128)S(1)}) custom-call(f32[5,125,8,128]{3,2,1,0:T(8,128)} %bitcast.3), custom_call_target="tpu_custom_call" | custom-call | flops 4096000 | bytes 5660672 | tf_op jit(solution)/shard_map/pallas_call | solution.py:557
  2.4 0.8 %collective-permute-start.1 = (f32[66,8,128]{2,1,0:T(8,128)S(1)}, f32[66,8,128]{2,1,0:T(8,128)S(1)}, u32[]{:S(2)}, u32[]{:S(2)}) collective-permute-start(f32[66,8,128]{2,1,0:T(8,128)S(1)} %get-tuple-element.24), channel_id=1, source_target_pairs={{0,1},{1,0},{2,3},{3,2},{4,5},{5,4},{6,7},{7,6},{8,9},{9,8},{10,11... | collective-permute-start | bytes 811016 | tf_op jit(solution)/shard_map/ppermute | solution.py:584
  3.2 2.0 %collective-permute-start.4 = (f32[65,8,128]{2,1,0:T(8,128)S(1)}, f32[65,8,128]{2,1,0:T(8,128)S(1)}, u32[]{:S(2)}, u32[]{:S(2)}) collective-permute-start(f32[65,8,128]{2,1,0:T(8,128)S(1)} %get-tuple-element.29), channel_id=1, source_target_pairs={{1,2},{2,1},{3,4},{4,3},{5,6},{6,5},{7,8},{8,7},{9,10},{10,9},{11,... | collective-permute-start | bytes 798728 | tf_op jit(solution)/shard_map/ppermute | solution.py:584
  5.2 1.3 %collective-permute-start = (f32[8,128]{1,0:T(8,128)S(1)}, f32[8,128]{1,0:T(8,128)S(1)}, u32[]{:S(2)}, u32[]{:S(2)}) collective-permute-start(f32[8,128]{1,0:T(8,128)S(1)} %get-tuple-element.23.eps), channel_id=1, source_target_pairs={{1,2},{2,1},{3,4},{4,3},{5,6},{6,5},{7,8},{8,7},{9,10},{10,9},{11,... | collective-permute-start | bytes 12296 | tf_op jit(solution)/shard_map/ppermute | solution.py:584
  6.4 7.0 %collective-permute-done.rkso = f32[8,128]{1,0:T(8,128)S(1)} collective-permute-done((f32[8,128]{1,0:T(8,128)S(1)}, f32[8,128]{1,0:T(8,128)S(1)}, u32[]{:S(2)}, u32[]{:S(2)}) %collective-permute-start) | collective-permute-done | bytes 4128 | tf_op jit(solution)/shard_map/ppermute | solution.py:584
  13.4 0.0 collective-permute-done.1.rse
  13.4 0.3 shard_map.32
  13.8 1.7 %collective-permute-start.2 = (f32[38,8,128]{2,1,0:T(8,128)S(1)}, f32[38,8,128]{2,1,0:T(8,128)S(1)}, u32[]{:S(2)}, u32[]{:S(2)}) collective-permute-start(f32[38,8,128]{2,1,0:T(8,128)S(1)} %get-tuple-element.25), channel_id=1, source_target_pairs={{0,16},{1,17},{2,18},{3,19},{4,20},{5,21},{6,22},{7,23},{8,24},{9,... | collective-permute-start | bytes 466952 | tf_op jit(solution)/shard_map/ppermute | solution.py:594
  15.5 2.1 %collective-permute-start.3 = (f32[38,8,128]{2,1,0:T(8,128)S(1)}, f32[38,8,128]{2,1,0:T(8,128)S(1)}, u32[]{:S(2)}, u32[]{:S(2)}) collective-permute-start(f32[38,8,128]{2,1,0:T(8,128)S(1)} %get-tuple-element.26), channel_id=1, source_target_pairs={{16,32},{17,33},{18,34},{19,35},{20,36},{21,37},{22,38},{23,39},{2... | collective-permute-start | bytes 466952 | tf_op jit(solution)/shard_map/ppermute | solution.py:594
  17.6 2.7 %shard_map.31 = (f32[5,125,8,128]{3,2,1,0:T(8,128)S(1)}, f32[5,125,8,128]{3,2,1,0:T(8,128)S(1)}, f32[5,125,8,128]{3,2,1,0:T(8,128)S(1)}) custom-call(f32[5,125,8,128]{3,2,1,0:T(8,128)S(1)} %get-tuple-element.20.state), custom_call_target="tpu_custom_call" | custom-call | flops 20480000 | bytes 10240000 | tf_op jit(solution)/shard_map/pallas_call | solution.py:557
  20.4 0.0 collective-permute-done.2.rce
  20.4 1.9 %collective-permute-done.3.rco = f32[38,8,128]{2,1,0:T(8,128)S(1)} collective-permute-done((f32[38,8,128]{2,1,0:T(8,128)S(1)}, f32[38,8,128]{2,1,0:T(8,128)S(1)}, u32[]{:S(2)}, u32[]{:S(2)}) %collective-permute-start.3) | collective-permute-done | bytes 155680 | tf_op jit(solution)/shard_map/ppermute | solution.py:594
  22.3 0.9 %shard_map.33 = (f32[125,8,128]{2,1,0:T(8,128)S(1)}, f32[5,125,8,128]{3,2,1,0:T(8,128)S(1)}, f32[35,8,128]{2,1,0:T(8,128)S(1)}, f32[35,8,128]{2,1,0:T(8,128)S(1)}) custom-call(f32[5,125,8,128]{3,2,1,0:T(8,128)S(1)} %get-tuple-element.22.gc, f32[8,128]{1,0:T(8,128)S(1)} %get-tuple-element.23.eps, f32[8,128]{1,0:T(8,128)S(1)} %collective-permute-done.rkso, ...), custom_call_target="tpu_custom_call" | custom-call | flops 8192000 | bytes 6508544 | tf_op jit(solution)/shard_map/pallas_call | solution.py:557
  23.2 0.0 collective-permute-done.4.rso
  23.2 0.7 %shard_map.34 = (f32[5,125,8,128]{3,2,1,0:T(8,128)S(1)}, f32[65,8,128]{2,1,0:T(8,128)S(1)}, f32[65,8,128]{2,1,0:T(8,128)S(1)}) custom-call(f32[5,125,8,128]{3,2,1,0:T(8,128)S(1)} %get-tuple-element.28.gs, f32[125,8,128]{2,1,0:T(8,128)S(1)} %get-tuple-element.27.visc, f32[66,8,128]{2,1,0:T(8,128)S(1)} %collective-permute-done.1.rse, ...), custom_call_target="tpu_custom_call" | custom-call | flops 8192000 | bytes 6701056 | tf_op jit(solution)/shard_map/pallas_call | solution.py:557
  23.9 0.1 collective-permute-start.7
  24.0 3.0 %collective-permute-start.8 = (f32[65,8,128]{2,1,0:T(8,128)S(1)}, f32[65,8,128]{2,1,0:T(8,128)S(1)}, u32[]{:S(2)}, u32[]{:S(2)}) collective-permute-start(f32[65,8,128]{2,1,0:T(8,128)S(1)} %get-tuple-element.36), channel_id=1, source_target_pairs={{1,2},{2,1},{3,4},{4,3},{5,6},{6,5},{7,8},{8,7},{9,10},{10,9},{11,... | collective-permute-start | bytes 798728 | tf_op jit(solution)/shard_map/ppermute | solution.py:584
  27.1 0.0 collective-permute-start.5
  27.1 3.0 %collective-permute-start.6 = (f32[35,8,128]{2,1,0:T(8,128)S(1)}, f32[35,8,128]{2,1,0:T(8,128)S(1)}, u32[]{:S(2)}, u32[]{:S(2)}) collective-permute-start(f32[35,8,128]{2,1,0:T(8,128)S(1)} %get-tuple-element.34), channel_id=1, source_target_pairs={{16,32},{17,33},{18,34},{19,35},{20,36},{21,37},{22,38},{23,39},{2... | collective-permute-start | bytes 430088 | tf_op jit(solution)/shard_map/ppermute | solution.py:594
  30.1 3.3 %shard_map.35 = (f32[5,125,8,128]{3,2,1,0:T(8,128)S(1)}, f32[125,8,128]{2,1,0:T(8,128)}) custom-call(f32[5,125,8,128]{3,2,1,0:T(8,128)S(1)} %get-tuple-element.21.gn, f32[125,8,128]{2,1,0:T(8,128)S(1)} %get-tuple-element.27.visc, f32[5,125,8,128]{3,2,1,0:T(8,128)S(1)} %get-tuple-element.30.fs, f32[5,125,8,128]{3,2,1,0:T(8,128)S(1)} %get-tuple-element.31.fc), custom_call_target="tpu_custom_call" | custom-call | flops 24576000 | bytes 11264000 | tf_op jit(solution)/shard_map/pallas_call | solution.py:557
  33.4 0.0 collective-permute-done.5.rbce
  33.4 6.4 %collective-permute-done.6.rbco = f32[35,8,128]{2,1,0:T(8,128)S(1)} collective-permute-done((f32[35,8,128]{2,1,0:T(8,128)S(1)}, f32[35,8,128]{2,1,0:T(8,128)S(1)}, u32[]{:S(2)}, u32[]{:S(2)}) %collective-permute-start.6) | collective-permute-done | bytes 143392 | tf_op jit(solution)/shard_map/ppermute | solution.py:594
  39.8 0.3 shard_map.36.res
  40.1 0.0 collective-permute-done.7.rbse
  40.1 0.0 collective-permute-done.8.rbso
  40.1 1.6 %shard_map.37 = f32[5,125,8,128]{3,2,1,0:T(8,128)} custom-call(f32[5,125,8,128]{3,2,1,0:T(8,128)S(1)} %shard_map.36.res, f32[65,8,128]{2,1,0:T(8,128)S(1)} %collective-permute-done.7.rbse, f32[65,8,128]{2,1,0:T(8,128)S(1)} %collective-permute-done.8.rbso), custom_call_target="tpu_custom_call" | custom-call | flops 8192000 | bytes 5652480 | tf_op jit(solution)/shard_map/pallas_call | solution.py:557
Async XLA Ops:
  2.4 11.0 %collective-permute-start.1 = (f32[66,8,128]{2,1,0:T(8,128)S(1)}, f32[66,8,128]{2,1,0:T(8,128)S(1)}, u32[]{:S(2)}, u32[]{:S(2)}) collective-permute-start(f32[66,8,128]{2,1,0:T(8,128)S(1)} %get-tuple-element.24), channel_id=1, source_target_pairs={{0,1},{1,0},{2,3},{3,2},{4,5},{5,4},{6,7},{7,6},{8,9},{9,8},{10,11... | collective-permute-start | bytes 811016 | tf_op jit(solution)/shard_map/ppermute | solution.py:584
  3.2 20.0 %collective-permute-start.4 = (f32[65,8,128]{2,1,0:T(8,128)S(1)}, f32[65,8,128]{2,1,0:T(8,128)S(1)}, u32[]{:S(2)}, u32[]{:S(2)}) collective-permute-start(f32[65,8,128]{2,1,0:T(8,128)S(1)} %get-tuple-element.29), channel_id=1, source_target_pairs={{1,2},{2,1},{3,4},{4,3},{5,6},{6,5},{7,8},{8,7},{9,10},{10,9},{11,... | collective-permute-start | bytes 798728 | tf_op jit(solution)/shard_map/ppermute | solution.py:584
  5.2 8.3 %collective-permute-start = (f32[8,128]{1,0:T(8,128)S(1)}, f32[8,128]{1,0:T(8,128)S(1)}, u32[]{:S(2)}, u32[]{:S(2)}) collective-permute-start(f32[8,128]{1,0:T(8,128)S(1)} %get-tuple-element.23.eps), channel_id=1, source_target_pairs={{1,2},{2,1},{3,4},{4,3},{5,6},{6,5},{7,8},{8,7},{9,10},{10,9},{11,... | collective-permute-start | bytes 12296 | tf_op jit(solution)/shard_map/ppermute | solution.py:584
  13.8 6.6 %collective-permute-start.2 = (f32[38,8,128]{2,1,0:T(8,128)S(1)}, f32[38,8,128]{2,1,0:T(8,128)S(1)}, u32[]{:S(2)}, u32[]{:S(2)}) collective-permute-start(f32[38,8,128]{2,1,0:T(8,128)S(1)} %get-tuple-element.25), channel_id=1, source_target_pairs={{0,16},{1,17},{2,18},{3,19},{4,20},{5,21},{6,22},{7,23},{8,24},{9,... | collective-permute-start | bytes 466952 | tf_op jit(solution)/shard_map/ppermute | solution.py:594
  15.5 6.8 %collective-permute-start.3 = (f32[38,8,128]{2,1,0:T(8,128)S(1)}, f32[38,8,128]{2,1,0:T(8,128)S(1)}, u32[]{:S(2)}, u32[]{:S(2)}) collective-permute-start(f32[38,8,128]{2,1,0:T(8,128)S(1)} %get-tuple-element.26), channel_id=1, source_target_pairs={{16,32},{17,33},{18,34},{19,35},{20,36},{21,37},{22,38},{23,39},{2... | collective-permute-start | bytes 466952 | tf_op jit(solution)/shard_map/ppermute | solution.py:594
  23.9 16.2 %collective-permute-start.7 = (f32[65,8,128]{2,1,0:T(8,128)S(1)}, f32[65,8,128]{2,1,0:T(8,128)S(1)}, u32[]{:S(2)}, u32[]{:S(2)}) collective-permute-start(f32[65,8,128]{2,1,0:T(8,128)S(1)} %get-tuple-element.35), channel_id=1, source_target_pairs={{0,1},{1,0},{2,3},{3,2},{4,5},{5,4},{6,7},{7,6},{8,9},{9,8},{10,11... | collective-permute-start | bytes 798728 | tf_op jit(solution)/shard_map/ppermute | solution.py:584
  24.0 16.1 %collective-permute-start.8 = (f32[65,8,128]{2,1,0:T(8,128)S(1)}, f32[65,8,128]{2,1,0:T(8,128)S(1)}, u32[]{:S(2)}, u32[]{:S(2)}) collective-permute-start(f32[65,8,128]{2,1,0:T(8,128)S(1)} %get-tuple-element.36), channel_id=1, source_target_pairs={{1,2},{2,1},{3,4},{4,3},{5,6},{6,5},{7,8},{8,7},{9,10},{10,9},{11,... | collective-permute-start | bytes 798728 | tf_op jit(solution)/shard_map/ppermute | solution.py:584
  27.1 6.4 %collective-permute-start.5 = (f32[35,8,128]{2,1,0:T(8,128)S(1)}, f32[35,8,128]{2,1,0:T(8,128)S(1)}, u32[]{:S(2)}, u32[]{:S(2)}) collective-permute-start(f32[35,8,128]{2,1,0:T(8,128)S(1)} %get-tuple-element.33), channel_id=1, source_target_pairs={{0,16},{1,17},{2,18},{3,19},{4,20},{5,21},{6,22},{7,23},{8,24},{9,... | collective-permute-start | bytes 430088 | tf_op jit(solution)/shard_map/ppermute | solution.py:594
  27.1 12.8 %collective-permute-start.6 = (f32[35,8,128]{2,1,0:T(8,128)S(1)}, f32[35,8,128]{2,1,0:T(8,128)S(1)}, u32[]{:S(2)}, u32[]{:S(2)}) collective-permute-start(f32[35,8,128]{2,1,0:T(8,128)S(1)} %get-tuple-element.34), channel_id=1, source_target_pairs={{16,32},{17,33},{18,34},{19,35},{20,36},{21,37},{22,38},{23,39},{2... | collective-permute-start | bytes 430088 | tf_op jit(solution)/shard_map/ppermute | solution.py:594

commit v2 on v1

--- a/solution.py
+++ b/solution.py
@@ -205,10 +205,14 @@
     return (jnp.where(even, second, first), jnp.where(even, first, second))
 
 
-def leave_span_kernel(source, so, se, eps_ref, state, work, sems):
-    reads = [pltpu.make_async_copy(source.at[v], state.at[v], sems.at[v]) for v in range(NV)]
-    for read in reads:
-        read.start()
+def sensor_kernel(source, eps, density, work, sem):
+    read = pltpu.make_async_copy(source.at[0], density, sem)
+    read.start()
+    read.wait()
+    eps[...] = sensor(density, work)
+
+
+def leave_span_kernel(state, so, se):
     _, j = row_ids()
     is_low = j == 0
     es = even_span()
@@ -221,20 +225,10 @@
         pack_span(leaving, is_low, es, se, so, v * SPAN_V)
         return carry
 
-    reads[0].wait()
-    eps = sensor(state, work)
-    eps_ref[...] = eps
-    se[SPAN_N] = eps
-    one(0, 0)
-
-    def later(v, carry):
-        pltpu.make_async_copy(source.at[v], state.at[v], sems.at[v]).wait()
-        return one(v, carry)
-
-    lax.fori_loop(1, NV, later, 0)
-
-
-def leave_chord_kernel(state, eps, rkso, rse, co, ce):
+    lax.fori_loop(0, NV, one, 0)
+
+
+def leave_chord_kernel(state, eps, rkce, rkco, se, co, ce, se_three, three):
     i, _ = row_ids()
     first_row = i == 0
     ec = even_chord()
@@ -248,14 +242,19 @@
         return carry
 
     lax.fori_loop(0, NV, one, 0)
-    before, after = sided(even_span(), rse[SPAN_N], rkso[...])
-    for ref in (co, ce):
-        ref[CHORD_N], ref[CHORD_N + 1], ref[CHORD_N + 2] = eps[...], before, after
-
-
-def sensor(state, work):
+    first, last = chord_ends()
+    behind, ahead = sided(ec, rkce[...], rkco[...])
+    values = (eps[...], jnp.where(first, 0.0, behind), jnp.where(last, 0.0, ahead))
+    for n, value in enumerate(values):
+        three[n] = value
+        se_three[SPAN_N + n] = value
+    for m in range(SPAN_N):
+        se_three[m] = se[m]
+
+
+def sensor(density, work):
     for axis in range(2):
-        origin = state.at[0] if axis == 0 else work
+        origin = density if axis == 0 else work
         for f in range(NF):
             points = line_points(axis, f)
             for p, value in zip(points, modal_line([origin[p] for p in points])):
@@ -309,31 +308,22 @@
     return (before + after, after - before)
 
 
-def gradient_kernel(state, gc, gs, gn, total_ref, diff_ref):
+def gradient_kernel(state, gc, gs):
     i, j = row_ids()
-    lane = lane_ids()
     is_low = j == 0
     sign_row = jnp.where(is_low, 1.0, -1.0)
 
     def one(v, carry):
-        def lines(axis, f):
-            return even_odd([state[v, p] for p in line_points(axis, f)])
-
-        for f in range(NF):
-            left, right = traces(lines(2, f))
-            total_ref[f], diff_ref[f] = neighbours_normal(left, right, 1.0, lane)
-        for axis, ref in ((0, gc), (1, gs), (2, gn)):
+        for axis, ref in ((0, gc), (1, gs)):
             for f in range(NF):
-                parts = lines(axis, f)
-                if axis == 2:
-                    total, diff = total_ref[f], diff_ref[f]
+                points = line_points(axis, f)
+                parts = even_odd([state[v, p] for p in points])
+                left, right = traces(parts)
+                if axis == 0:
+                    total, diff = neighbours_chord(left, right, 1.0, i)
                 else:
-                    left, right = traces(parts)
-                    if axis == 0:
-                        total, diff = neighbours_chord(left, right, 1.0, i)
-                    else:
-                        total, diff = neighbours_span(left, right, is_low, sign_row)
-                for p, value in zip(line_points(axis, f), slope(parts, total, diff)):
+                    total, diff = neighbours_span(left, right, is_low, sign_row)
+                for p, value in zip(points, slope(parts, total, diff)):
                     ref[v, p] = value
         return carry
 
@@ -376,11 +366,42 @@
                 visc[25 * a + 5 * b + c] = mul(halves[c][0], low) + mul(halves[c][1], high)
 
 
+def chord_send_kernel(gc, three, rkso, rse, visc, bco, bce):
+    i, _ = row_ids()
+    first_row = i == 0
+    es, ec = even_span(), even_chord()
+    viscosity_into(
+        visc, *((three[n],) + sided(es, rse[SPAN_N + n], rkso[n]) for n in range(3))
+    )
+
+    def one(v, carry):
+        def leaving(f):
+            left, right = traces(even_odd([visc[p] * gc[v, p] for p in line_points(0, f)]))
+            return jnp.where(first_row, left, right)
+
+        pack_chord(leaving, i, ec, bce, bco, v * CHORD_V)
+        return carry
+
+    lax.fori_loop(0, NV, one, 0)
+    share = 0.5 * LEFT * CORR_L
+
+    def factor(f):
+        e0, e1, o0, o1, c = even_odd([visc[p] for p in line_points(0, f)])
+        even = (
+            mul(0.5 * (share[0] + share[4]), e0)
+            + mul(0.5 * (share[1] + share[3]), e1)
+            + mul(share[2], c)
+        )
+        odd = mul(0.5 * (share[0] - share[4]), o0) + mul(0.5 * (share[1] - share[3]), o1)
+        return jnp.where(first_row, odd + even, odd - even)
+
+    pack_chord(factor, i, ec, bce, bco, CHORD_N)
+
+
 def span_flux_kernel(gs, visc, rse, rso, fs, bso, bse):
     _, j = row_ids()
     is_low = j == 0
-    es, ec = even_span(), even_chord()
-
+    es = even_span()
     weights = span_weights(is_low)
 
     def one(v, carry):
@@ -406,94 +427,87 @@
     lax.fori_loop(0, NV, one, 0)
 
 
-def chord_flux_kernel(gc, eps, rkso, rse, rce, rco, visc, fc, bco, bce):
-    i, _ = row_ids()
-    first_row = i == 0
-    es, ec = even_span(), even_chord()
-    before, after = sided(es, rse[SPAN_N], rkso[...])
-    first, last = chord_ends()
-    low, high = [], []
-    for n in range(3):
-        behind, ahead = sided(ec, rce[CHORD_N + n], rco[CHORD_N + n])
-        low.append(jnp.where(first, 0.0, behind))
-        high.append(jnp.where(last, 0.0, ahead))
-    viscosity_into(visc, (eps[...], before, after), low, high)
-    weights = chord_weights(i)
-
-    def one(v, carry):
-        received = {}
-
-        def leaving(f):
-            m, q = f // 4, f % 4
-            if m not in received:
-                base = v * CHORD_V + m
-                first, second = rce[base], rco[base]
-                received[m] = (jnp.where(ec, second, first), jnp.where(ec, first, second))
-            edge = open_chord(received[m][0], received[m][1], q, i)
-            values = []
-            for k, p in enumerate(line_points(0, f)):
-                value = visc[p] * (gc[v, p] + weights[k] * edge)
-                fc[v, p] = value
-                values.append(value)
-            left, right = traces(even_odd(values))
-            return jnp.where(first_row, left, right)
-
-        pack_chord(leaving, i, ec, bce, bco, v * CHORD_V)
-        return carry
-
-    lax.fori_loop(0, NV, one, 0)
-
-
-def divergence_kernel(gn, visc, fs, fc, res, visc_out, total_ref, diff_ref, sem):
+def inner_kernel(state, visc, fs, gc, rce, rco, res, visc_out, total_ref, diff_ref, flux, sem):
     write = pltpu.make_async_copy(visc, visc_out, sem)
     write.start()
     i, j = row_ids()
     lane = lane_ids()
     is_low = j == 0
     sign_row = jnp.where(is_low, 1.0, -1.0)
-
-    def one(v, carry):
-        def normal_flux(f):
-            return even_odd([visc[p] * gn[v, p] for p in line_points(2, f)])
+    ec = even_chord()
+    weights = chord_weights(i)
+
+    def one(v, carry):
+        received = {}
+
+        def across(c):
+            plane = {}
+            for b in range(5):
+                f = 5 * b + c
+                m, q = f // 4, f % 4
+                if m not in received:
+                    at = v * CHORD_V + m
+                    received[m] = sided(ec, rce[at], rco[at])
+                edge = open_chord(*received[m], q, i)
+                points = line_points(0, f)
+                parts = even_odd(
+                    [visc[p] * (gc[v, p] + weights[k] * edge) for k, p in enumerate(points)]
+                )
+                total, diff = neighbours_chord(*traces(parts), -1.0, i)
+                plane.update(zip(points, slope(parts, total, diff)))
+            for a in range(5):
+                points = line_points(1, 5 * a + c)
+                parts = even_odd([fs[v, p] for p in points])
+                total, diff = neighbours_span(*traces(parts), is_low, sign_row)
+                for p, value in zip(points, slope(parts, total, diff)):
+                    res[v, p] = plane[p] + value
 
         for f in range(NF):
-            left, right = traces(normal_flux(f))
-            total_ref[f], diff_ref[f] = neighbours_normal(left, right, -1.0, lane)
-        for axis, ref in ((0, fc), (1, fs), (2, gn)):
-            for f in range(NF):
-                points = line_points(axis, f)
-                if axis == 2:
-                    parts = normal_flux(f)
-                    total, diff = total_ref[f], diff_ref[f]
-                else:
-                    parts = even_odd([ref[v, p] for p in points])
-                    left, right = traces(parts)
-                    if axis == 0:
-                        total, diff = neighbours_chord(left, right, -1.0, i)
-                    else:
-                        total, diff = neighbours_span(left, right, is_low, sign_row)
-                for p, value in zip(points, slope(parts, total, diff)):
-                    res[v, p] = value if axis == 0 else res[v, p] + value
+            ends = traces(even_odd([state[v, p] for p in line_points(2, f)]))
+            total_ref[f], diff_ref[f] = neighbours_normal(*ends, 1.0, lane)
+        across(0)
+        across(1)
+        for f in range(NF):
+            points = line_points(2, f)
+            parts = even_odd([state[v, p] for p in points])
+            values = slope(parts, total_ref[f], diff_ref[f])
+            values = [visc[p] * value for p, value in zip(points, values)]
+            for p, value in zip(points, values):
+                flux[p] = value
+            ends = traces(even_odd(values))
+            total_ref[NF + f], diff_ref[NF + f] = neighbours_normal(*ends, -1.0, lane)
+        across(2)
+        across(3)
+        across(4)
+        for f in range(NF):
+            points = line_points(2, f)
+            parts = even_odd([flux[p] for p in points])
+            values = slope(parts, total_ref[NF + f], diff_ref[NF + f])
+            for p, value in zip(points, values):
+                res[v, p] = res[v, p] + value
         return carry
 
     lax.fori_loop(0, NV, one, 0)
     write.wait()
 
 
-def close_chord_kernel(res, rbce, rbco, out, edge):
+def close_chord_kernel(res, ce, co, rbce, rbco, out):
     i, _ = row_ids()
     ec = even_chord()
     weights = chord_weights(i)
 
     def one(v, carry):
         for m in range(CHORD_V):
-            first, second = rbce[v * CHORD_V + m], rbco[v * CHORD_V + m]
-            behind, ahead = jnp.where(ec, second, first), jnp.where(ec, first, second)
+            at = v * CHORD_V + m
+            behind, ahead = sided(
+                ec,
+                rbce[at] + rbce[CHORD_N + m] * ce[at],
+                rbco[at] + rbco[CHORD_N + m] * co[at],
+            )
             for f in range(4 * m, min(4 * m + 4, NF)):
-                edge[f] = open_chord(behind, ahead, f % 4, i)
-        for f in range(NF):
-            for k, p in enumerate(line_points(0, f)):
-                out[v, p] = res[v, p] + weights[k] * edge[f]
+                edge = open_chord(behind, ahead, f % 4, i)
+                for k, p in enumerate(line_points(0, f)):
+                    out[v, p] = res[v, p] + weights[k] * edge
         return carry
 
     lax.fori_loop(0, NV, one, 0)
@@ -595,26 +609,30 @@
 
     dma = pltpu.SemaphoreType.DMA
     u = state.reshape(NV, 125, ROWS, LANES)
-    so, se, eps, near = call(
-        leave_span_kernel,
-        [vec(SPAN_N), vec(SPAN_N + 1), vec(), vec(NV, 125)],
+    (eps,) = call(
+        sensor_kernel,
+        [vec()],
         [pltpu.with_memory_space_constraint(u, pltpu.HBM)],
-        [held(125), dma((NV,))],
+        [held(125), held(125), dma(())],
         far_in=(0,),
     )
-    rkso = span_swap(eps, 1)
+    rkco = chord_swap(eps, 1)
+    rkce = chord_swap(eps, 0)
+    so, se = call(leave_span_kernel, [vec(SPAN_N), vec(SPAN_N)], [u])
+    rso = span_swap(so, 1)
+    co, ce, se, three = call(
+        leave_chord_kernel,
+        [vec(CHORD_N), vec(CHORD_N), vec(SPAN_N + 3), vec(3)],
+        [u, eps, rkce, rkco, se],
+    )
     rse = span_swap(se, 0)
-    rso = span_swap(so, 1)
-    co, ce = call(leave_chord_kernel, [vec(CHORD_N + 3), vec(CHORD_N + 3)], [near, eps, rkso, rse])
+    rkso = span_swap(three, 1)
     rco = chord_swap(co, 1)
-    rce = chord_swap(ce, 0)
-    gc, gs, gn = call(
-        gradient_kernel, [vec(NV, 125)] * 3, [near], [held(NF), held(NF)], cycles=5000
-    )
-    visc, fc, bco, bce = call(
-        chord_flux_kernel,
-        [vec(125), vec(NV, 125), vec(CHORD_N), vec(CHORD_N)],
-        [gc, eps, rkso, rse, rce, rco],
+    gc, gs = call(gradient_kernel, [vec(NV, 125)] * 2, [u], cycles=4000)
+    visc, bco, bce = call(
+        chord_send_kernel,
+        [vec(125), vec(CHORD_N + CHORD_V), vec(CHORD_N + CHORD_V)],
+        [gc, three, rkso, rse],
         cycles=2000,
     )
     rbco = chord_swap(bco, 1)
@@ -625,17 +643,18 @@
         cycles=2000,
     )
     rbso = span_swap(bso, 1)
+    rbce = chord_swap(bce, 0)
+    rce = chord_swap(ce, 0)
     rbse = span_swap(bse, 0)
-    rbce = chord_swap(bce, 0)
     res, visc_out = call(
-        divergence_kernel,
+        inner_kernel,
         [vec(NV, 125), vec(125)],
-        [gn, visc, fs, fc],
-        [held(NF), held(NF), dma(())],
+        [u, visc, fs, gc, rce, rco],
+        [held(2 * NF), held(2 * NF), held(125), dma(())],
         cycles=6000,
         far_out=(1,),
     )
-    (res,) = call(close_chord_kernel, [vec(NV, 125)], [res, rbce, rbco], [held(NF)], cycles=1000)
+    (res,) = call(close_chord_kernel, [vec(NV, 125)], [res, ce, co, rbce, rbco], cycles=1000)
     (out,) = call(
         close_span_kernel,
         [vec(NV, 125)],

time: 41.9 us -> 48 us (1.15)
  waiting for transfers between devices: 15.4 us -> 20.4 us
  starting transfers between devices: 14 us -> 14.9 us
    ppermute x4 -> x6, waiting for transfers between devices: 8.32 us -> 14.9 us  [chord_swap(): return lax.ppermute(array, ('chord', 'span'), route)]
    ppermute x5, waiting for transfers between devices: 7.05 us -> 5.42 us  [span_swap(): return lax.ppermute(array, 'span', paired(spans, odd, True))]
    ppermute x4 -> x6, starting transfers between devices: 6.88 us -> 7.43 us  [chord_swap(): return lax.ppermute(array, ('chord', 'span'), route)]
    pallas_call x8 -> x9, Pallas kernels: 11.6 us -> 11.8 us  [call(): pl.pallas_call(kernel, out_shape=outs, in_specs=[hbm if n in far_in else...]
  transfers between devices with their start and end apart: 9 -> 11, of which waited for: 3 -> 3; matrix products, arithmetic and copies ran while one was open for 0% -> 0% of each run, Pallas kernels for 18% -> 17%
where the time goes in v2:
time: 48 us; the launch traced here: 47.8 us
  waiting for transfers between devices  20.4 us (42%)
  starting transfers between devices  14.9 us (31%)
  Pallas kernels  11.8 us (25%)
  between operations  0.74 us (2%)
    ppermute x6, waiting for transfers between devices, chord_swap(): return lax.ppermute(array, ('chord', 'span'), route)  14.9 us
    pallas_call x9, Pallas kernels, call(): pl.pallas_call(kernel, out_shape=outs, in_specs=[hbm if n in far_in else...  11.8 us
    ppermute x5, starting transfers between devices, span_swap(): return lax.ppermute(array, 'span', paired(spans, odd, True))  7.51 us
    ppermute x6, starting transfers between devices, chord_swap(): return lax.ppermute(array, ('chord', 'span'), route)  7.43 us
    ppermute x5, waiting for transfers between devices, span_swap(): return lax.ppermute(array, 'span', paired(spans, odd, True))  5.42 us
  transfers between devices with their start and end apart: 11, of which 3 were waited for; matrix products, arithmetic and copies ran while one was open for 0% of the time, Pallas kernels for 17%

profile of v2, /device:TPU:15, one launch (start us, length us, event | category | flops | bytes accessed | tf_op | source)
XLA Modules:
  0.0 47.8 jit_solution(5492745132477070987)
XLA Ops:
  0.6 0.0 copy-start
  0.6 1.6 %shard_map.31.eps = f32[8,128]{1,0:T(8,128)S(1)} custom-call(f32[5,125,8,128]{3,2,1,0:T(8,128)} %bitcast.3), custom_call_target="tpu_custom_call" | custom-call | flops 4096000 | bytes 2564096 | tf_op jit(solution)/shard_map/pallas_call | solution.py:571
  2.2 1.7 %collective-permute-start = (f32[8,128]{1,0:T(8,128)S(1)}, f32[8,128]{1,0:T(8,128)S(1)}, u32[]{:S(2)}, u32[]{:S(2)}) collective-permute-start(f32[8,128]{1,0:T(8,128)S(1)} %shard_map.31.eps), channel_id=1, source_target_pairs={{0,16},{1,17},{2,18},{3,19},{4,20},{5,21},{6,22},{7,23},{8,24},{9,... | collective-permute-start | bytes 12296 | tf_op jit(solution)/shard_map/ppermute | solution.py:608
  3.9 2.1 %collective-permute-start.1 = (f32[8,128]{1,0:T(8,128)S(1)}, f32[8,128]{1,0:T(8,128)S(1)}, u32[]{:S(2)}, u32[]{:S(2)}) collective-permute-start(f32[8,128]{1,0:T(8,128)S(1)} %shard_map.31.eps), channel_id=1, source_target_pairs={{16,32},{17,33},{18,34},{19,35},{20,36},{21,37},{22,38},{23,39},{2... | collective-permute-start | bytes 12296 | tf_op jit(solution)/shard_map/ppermute | solution.py:608
  6.0 0.3 shard_map.32
  6.4 0.0 collective-permute-done.rkce
  6.4 2.1 %collective-permute-done.1.rkco = f32[8,128]{1,0:T(8,128)S(1)} collective-permute-done((f32[8,128]{1,0:T(8,128)S(1)}, f32[8,128]{1,0:T(8,128)S(1)}, u32[]{:S(2)}, u32[]{:S(2)}) %collective-permute-start.1) | collective-permute-done | bytes 4128 | tf_op jit(solution)/shard_map/ppermute | solution.py:608
  8.5 0.3 shard_map.33
  8.8 2.2 %collective-permute-start.3 = (f32[68,8,128]{2,1,0:T(8,128)S(1)}, f32[68,8,128]{2,1,0:T(8,128)S(1)}, u32[]{:S(2)}, u32[]{:S(2)}) collective-permute-start(f32[68,8,128]{2,1,0:T(8,128)S(1)} %get-tuple-element.21), channel_id=1, source_target_pairs={{0,1},{1,0},{2,3},{3,2},{4,5},{5,4},{6,7},{7,6},{8,9},{9,8},{10,11... | collective-permute-start | bytes 835592 | tf_op jit(solution)/shard_map/ppermute | solution.py:598
  11.0 2.0 %collective-permute-start.4 = (f32[65,8,128]{2,1,0:T(8,128)S(1)}, f32[65,8,128]{2,1,0:T(8,128)S(1)}, u32[]{:S(2)}, u32[]{:S(2)}) collective-permute-start(f32[65,8,128]{2,1,0:T(8,128)S(1)} %get-tuple-element.24), channel_id=1, source_target_pairs={{1,2},{2,1},{3,4},{4,3},{5,6},{6,5},{7,8},{8,7},{9,10},{10,9},{11,... | collective-permute-start | bytes 798728 | tf_op jit(solution)/shard_map/ppermute | solution.py:598
  13.0 0.0 collective-permute-start.5
  13.0 1.3 %collective-permute-start.2 = (f32[3,8,128]{2,1,0:T(8,128)S(1)}, f32[3,8,128]{2,1,0:T(8,128)S(1)}, u32[]{:S(2)}, u32[]{:S(2)}) collective-permute-start(f32[3,8,128]{2,1,0:T(8,128)S(1)} %get-tuple-element.20.three), channel_id=1, source_target_pairs={{1,2},{2,1},{3,4},{4,3},{5,6},{6,5},{7,8},{8,7},{9,10},{10,9},{11,... | collective-permute-start | bytes 36872 | tf_op jit(solution)/shard_map/ppermute | solution.py:598
  14.3 1.8 %shard_map.30 = (f32[5,125,8,128]{3,2,1,0:T(8,128)S(1)}, f32[5,125,8,128]{3,2,1,0:T(8,128)S(1)}) custom-call(f32[5,125,8,128]{3,2,1,0:T(8,128)S(1)} %bitcast.6), custom_call_target="tpu_custom_call" | custom-call | flops 16384000 | bytes 7680000 | tf_op jit(solution)/shard_map/pallas_call | solution.py:571
  16.1 5.4 %collective-permute-done.2.rkso = f32[3,8,128]{2,1,0:T(8,128)S(1)} collective-permute-done((f32[3,8,128]{2,1,0:T(8,128)S(1)}, f32[3,8,128]{2,1,0:T(8,128)S(1)}, u32[]{:S(2)}, u32[]{:S(2)}) %collective-permute-start.2) | collective-permute-done | bytes 12320 | tf_op jit(solution)/shard_map/ppermute | solution.py:598
  21.5 0.0 collective-permute-done.3.rse
  21.5 0.7 %shard_map.34 = (f32[125,8,128]{2,1,0:T(8,128)S(1)}, f32[42,8,128]{2,1,0:T(8,128)S(1)}, f32[42,8,128]{2,1,0:T(8,128)S(1)}) custom-call(f32[5,125,8,128]{3,2,1,0:T(8,128)S(1)} %get-tuple-element.18.gc, f32[3,8,128]{2,1,0:T(8,128)S(1)} %get-tuple-element.20.three, f32[3,8,128]{2,1,0:T(8,128)S(1)} %collective-permute-done.2.rkso, ...), custom_call_target="tpu_custom_call" | custom-call | flops 8192000 | bytes 3719168 | tf_op jit(solution)/shard_map/pallas_call | solution.py:571
  22.2 0.0 collective-permute-done.4.rso
  22.2 0.7 %shard_map.35 = (f32[5,125,8,128]{3,2,1,0:T(8,128)S(1)}, f32[65,8,128]{2,1,0:T(8,128)S(1)}, f32[65,8,128]{2,1,0:T(8,128)S(1)}) custom-call(f32[5,125,8,128]{3,2,1,0:T(8,128)S(1)} %get-tuple-element.23.gs, f32[125,8,128]{2,1,0:T(8,128)S(1)} %get-tuple-element.22.visc, f32[68,8,128]{2,1,0:T(8,128)S(1)} %collective-permute-done.3.rse, ...), custom_call_target="tpu_custom_call" | custom-call | flops 8192000 | bytes 6709248 | tf_op jit(solution)/shard_map/pallas_call | solution.py:571
  22.9 2.1 %collective-permute-start.10 = (f32[65,8,128]{2,1,0:T(8,128)S(1)}, f32[65,8,128]{2,1,0:T(8,128)S(1)}, u32[]{:S(2)}, u32[]{:S(2)}) collective-permute-start(f32[65,8,128]{2,1,0:T(8,128)S(1)} %get-tuple-element.32), channel_id=1, source_target_pairs={{1,2},{2,1},{3,4},{4,3},{5,6},{6,5},{7,8},{8,7},{9,10},{10,9},{11,... | collective-permute-start | bytes 798728 | tf_op jit(solution)/shard_map/ppermute | solution.py:598
  25.0 0.0 collective-permute-start.9
  25.0 0.0 collective-permute-start.7
  25.0 3.0 %collective-permute-start.8 = (f32[42,8,128]{2,1,0:T(8,128)S(1)}, f32[42,8,128]{2,1,0:T(8,128)S(1)}, u32[]{:S(2)}, u32[]{:S(2)}) collective-permute-start(f32[42,8,128]{2,1,0:T(8,128)S(1)} %get-tuple-element.30), channel_id=1, source_target_pairs={{16,32},{17,33},{18,34},{19,35},{20,36},{21,37},{22,38},{23,39},{2... | collective-permute-start | bytes 516104 | tf_op jit(solution)/shard_map/ppermute | solution.py:608
  28.0 0.0 collective-permute-done.5.rce
  28.0 0.5 %collective-permute-start.6 = (f32[35,8,128]{2,1,0:T(8,128)S(1)}, f32[35,8,128]{2,1,0:T(8,128)S(1)}, u32[]{:S(2)}, u32[]{:S(2)}) collective-permute-start(f32[35,8,128]{2,1,0:T(8,128)S(1)} %get-tuple-element.27.co), channel_id=1, source_target_pairs={{16,32},{17,33},{18,34},{19,35},{20,36},{21,37},{22,38},{23,39},{2... | collective-permute-start | bytes 430088 | tf_op jit(solution)/shard_map/ppermute | solution.py:608
  28.6 12.9 %collective-permute-done.6.rco = f32[35,8,128]{2,1,0:T(8,128)S(1)} collective-permute-done((f32[35,8,128]{2,1,0:T(8,128)S(1)}, f32[35,8,128]{2,1,0:T(8,128)S(1)}, u32[]{:S(2)}, u32[]{:S(2)}) %collective-permute-start.6) | collective-permute-done | bytes 143392 | tf_op jit(solution)/shard_map/ppermute | solution.py:608
  41.4 4.4 %shard_map.36 = (f32[5,125,8,128]{3,2,1,0:T(8,128)S(1)}, f32[125,8,128]{2,1,0:T(8,128)}) custom-call(f32[5,125,8,128]{3,2,1,0:T(8,128)S(1)} %bitcast.7, f32[125,8,128]{2,1,0:T(8,128)S(1)} %get-tuple-element.22.visc, f32[5,125,8,128]{3,2,1,0:T(8,128)S(1)} %get-tuple-element.25.fs, f32[5,125,8,128]{3,2,1,0:T(8,128)S(1)} %get-tuple-element.18.gc, ...), custom_call_target="tpu_custom_call" | custom-call | flops 24576000 | bytes 11550720 | tf_op jit(solution)/shard_map/pallas_call | solution.py:571
  45.8 0.0 collective-permute-done.7.rbce
  45.8 0.0 collective-permute-done.8.rbco
  45.8 0.3 shard_map.37.res
  46.2 0.0 collective-permute-done.10.rbso
  46.2 0.0 collective-permute-done.9.rbse
  46.2 1.6 %shard_map.38 = f32[5,125,8,128]{3,2,1,0:T(8,128)} custom-call(f32[5,125,8,128]{3,2,1,0:T(8,128)S(1)} %shard_map.37.res, f32[65,8,128]{2,1,0:T(8,128)S(1)} %collective-permute-done.9.rbse, f32[65,8,128]{2,1,0:T(8,128)S(1)} %collective-permute-done.10.rbso), custom_call_target="tpu_custom_call" | custom-call | flops 8192000 | bytes 5652480 | tf_op jit(solution)/shard_map/pallas_call | solution.py:571
  (1 shorter events, 0.0 us)
Async XLA Ops:
  0.6 5.4 %copy-start = (f32[5,125,4,2,128]{4,3,2,1,0:T(2,128)S(1)}, f32[5,125,4,2,128]{4,3,2,1,0:T(2,128)}, u32[]{:S(2)}) copy-start(f32[5,125,4,2,128]{4,3,2,1,0:T(2,128)} %param.1) | copy-start | bytes 7680004
  2.2 4.2 %collective-permute-start = (f32[8,128]{1,0:T(8,128)S(1)}, f32[8,128]{1,0:T(8,128)S(1)}, u32[]{:S(2)}, u32[]{:S(2)}) collective-permute-start(f32[8,128]{1,0:T(8,128)S(1)} %shard_map.31.eps), channel_id=1, source_target_pairs={{0,16},{1,17},{2,18},{3,19},{4,20},{5,21},{6,22},{7,23},{8,24},{9,... | collective-permute-start | bytes 12296 | tf_op jit(solution)/shard_map/ppermute | solution.py:608
  3.9 4.6 %collective-permute-start.1 = (f32[8,128]{1,0:T(8,128)S(1)}, f32[8,128]{1,0:T(8,128)S(1)}, u32[]{:S(2)}, u32[]{:S(2)}) collective-permute-start(f32[8,128]{1,0:T(8,128)S(1)} %shard_map.31.eps), channel_id=1, source_target_pairs={{16,32},{17,33},{18,34},{19,35},{20,36},{21,37},{22,38},{23,39},{2... | collective-permute-start | bytes 12296 | tf_op jit(solution)/shard_map/ppermute | solution.py:608
  8.8 12.6 %collective-permute-start.3 = (f32[68,8,128]{2,1,0:T(8,128)S(1)}, f32[68,8,128]{2,1,0:T(8,128)S(1)}, u32[]{:S(2)}, u32[]{:S(2)}) collective-permute-start(f32[68,8,128]{2,1,0:T(8,128)S(1)} %get-tuple-element.21), channel_id=1, source_target_pairs={{0,1},{1,0},{2,3},{3,2},{4,5},{5,4},{6,7},{7,6},{8,9},{9,8},{10,11... | collective-permute-start | bytes 835592 | tf_op jit(solution)/shard_map/ppermute | solution.py:598
  11.0 11.2 %collective-permute-start.4 = (f32[65,8,128]{2,1,0:T(8,128)S(1)}, f32[65,8,128]{2,1,0:T(8,128)S(1)}, u32[]{:S(2)}, u32[]{:S(2)}) collective-permute-start(f32[65,8,128]{2,1,0:T(8,128)S(1)} %get-tuple-element.24), channel_id=1, source_target_pairs={{1,2},{2,1},{3,4},{4,3},{5,6},{6,5},{7,8},{8,7},{9,10},{10,9},{11,... | collective-permute-start | bytes 798728 | tf_op jit(solution)/shard_map/ppermute | solution.py:598
  13.0 15.0 %collective-permute-start.5 = (f32[35,8,128]{2,1,0:T(8,128)S(1)}, f32[35,8,128]{2,1,0:T(8,128)S(1)}, u32[]{:S(2)}, u32[]{:S(2)}) collective-permute-start(f32[35,8,128]{2,1,0:T(8,128)S(1)} %get-tuple-element.26.ce), channel_id=1, source_target_pairs={{0,16},{1,17},{2,18},{3,19},{4,20},{5,21},{6,22},{7,23},{8,24},{9,... | collective-permute-start | bytes 430088 | tf_op jit(solution)/shard_map/ppermute | solution.py:608
  13.0 8.5 %collective-permute-start.2 = (f32[3,8,128]{2,1,0:T(8,128)S(1)}, f32[3,8,128]{2,1,0:T(8,128)S(1)}, u32[]{:S(2)}, u32[]{:S(2)}) collective-permute-start(f32[3,8,128]{2,1,0:T(8,128)S(1)} %get-tuple-element.20.three), channel_id=1, source_target_pairs={{1,2},{2,1},{3,4},{4,3},{5,6},{6,5},{7,8},{8,7},{9,10},{10,9},{11,... | collective-permute-start | bytes 36872 | tf_op jit(solution)/shard_map/ppermute | solution.py:598
  22.9 23.3 %collective-permute-start.10 = (f32[65,8,128]{2,1,0:T(8,128)S(1)}, f32[65,8,128]{2,1,0:T(8,128)S(1)}, u32[]{:S(2)}, u32[]{:S(2)}) collective-permute-start(f32[65,8,128]{2,1,0:T(8,128)S(1)} %get-tuple-element.32), channel_id=1, source_target_pairs={{1,2},{2,1},{3,4},{4,3},{5,6},{6,5},{7,8},{8,7},{9,10},{10,9},{11,... | collective-permute-start | bytes 798728 | tf_op jit(solution)/shard_map/ppermute | solution.py:598
  25.0 21.2 %collective-permute-start.9 = (f32[65,8,128]{2,1,0:T(8,128)S(1)}, f32[65,8,128]{2,1,0:T(8,128)S(1)}, u32[]{:S(2)}, u32[]{:S(2)}) collective-permute-start(f32[65,8,128]{2,1,0:T(8,128)S(1)} %get-tuple-element.31), channel_id=1, source_target_pairs={{0,1},{1,0},{2,3},{3,2},{4,5},{5,4},{6,7},{7,6},{8,9},{9,8},{10,11... | collective-permute-start | bytes 798728 | tf_op jit(solution)/shard_map/ppermute | solution.py:598
  25.0 20.8 %collective-permute-start.7 = (f32[42,8,128]{2,1,0:T(8,128)S(1)}, f32[42,8,128]{2,1,0:T(8,128)S(1)}, u32[]{:S(2)}, u32[]{:S(2)}) collective-permute-start(f32[42,8,128]{2,1,0:T(8,128)S(1)} %get-tuple-element.29), channel_id=1, source_target_pairs={{0,16},{1,17},{2,18},{3,19},{4,20},{5,21},{6,22},{7,23},{8,24},{9,... | collective-permute-start | bytes 516104 | tf_op jit(solution)/shard_map/ppermute | solution.py:608
  25.0 20.8 %collective-permute-start.8 = (f32[42,8,128]{2,1,0:T(8,128)S(1)}, f32[42,8,128]{2,1,0:T(8,128)S(1)}, u32[]{:S(2)}, u32[]{:S(2)}) collective-permute-start(f32[42,8,128]{2,1,0:T(8,128)S(1)} %get-tuple-element.30), channel_id=1, source_target_pairs={{16,32},{17,33},{18,34},{19,35},{20,36},{21,37},{22,38},{23,39},{2... | collective-permute-start | bytes 516104 | tf_op jit(solution)/shard_map/ppermute | solution.py:608
  28.0 13.4 %collective-permute-start.6 = (f32[35,8,128]{2,1,0:T(8,128)S(1)}, f32[35,8,128]{2,1,0:T(8,128)S(1)}, u32[]{:S(2)}, u32[]{:S(2)}) collective-permute-start(f32[35,8,128]{2,1,0:T(8,128)S(1)} %get-tuple-element.27.co), channel_id=1, source_target_pairs={{16,32},{17,33},{18,34},{19,35},{20,36},{21,37},{22,38},{23,39},{2... | collective-permute-start | bytes 430088 | tf_op jit(solution)/shard_map/ppermute | solution.py:608
